TPU v7x, 32 devices: a whole 2x2x4 slice. The times are simulated.
32 devices in a mesh: tile: 8 (over y, x, core), trc: 4 (over z).
Axes of the slice: x: 2, y: 2, z: 4, core: 2. Of those that a mesh axis runs over, the one named last changes fastest.
Arguments:
- tracers: float32 [512, 32, 2, 128], P('trc', 'tile'), may hold values from 0.05 to 2
- courant: float32 [3, 32, 2, 128], P(None, 'tile', None, 'trc'), may hold values from -6 to 6
- shear: float32 [3, 32, 2, 128], P(None, 'tile', None, 'trc'), may hold values from -8 to 8
- offsets: int32 [3, 32, 2, 128], P(None, 'tile'), may hold values from -1 to 0
- seam_flips: int32 [8], replicated, may hold values from 0 to 1
- kernel: float32 [32, 32], replicated, may hold values from 0.0005 to 0.004
- coag_target: int32 [32, 32], replicated, may hold values from 0 to 31, as said below
Outputs:
- updated: float32 [512, 32, 2, 128], P('trc', 'tile')
Inputs may be any that keep to these rules, and one draw needn't show every extreme that they name: coag_target[i, j] lies between max(i, j) and 31.
All inputs are finite; a program needn't handle non-finite values.
Results may differ from a plain program's by a relative error of at most 0.00014.
Values sent between devices are 32-bit elements; how exact they have to be, the bound alone decides.
No kernel may reach another device: no remote copies, remote signals or barrier semaphores. Data moves between devices by JAX's collectives and lax.ppermute only.
A program may use at most 64 MiB of HBM per device.

v0:
```python
import jax
import jax.numpy as jnp
from jax import lax
from jax.sharding import PartitionSpec as P

BINS = 32
COMPS = 16
ITER = 3


precise = lax.Precision.HIGHEST


def with_halo(cells, sides, width):
    for axis, dim in sides:
        count = lax.axis_size(axis)
        head = lax.slice_in_dim(cells, 0, width, axis=dim)
        tail = lax.slice_in_dim(cells, cells.shape[dim] - width, cells.shape[dim], axis=dim)
        cells = jnp.concatenate(
            [
                lax.ppermute(tail, axis, [(i, (i + 1) % count) for i in range(count)]),
                cells,
                lax.ppermute(head, axis, [((i + 1) % count, i) for i in range(count)]),
            ],
            axis=dim,
        )
    return cells


def fractions(courant, shear):
    fraction = jnp.full(courant.shape, 0.5, jnp.float32)
    for repeat in range(ITER):
        fraction = jax.nn.sigmoid(courant + shear * (fraction - 0.5))
    return fraction


def cubic_taps(fraction, offsets):
    first_node = -fraction * (fraction - 1.0) * (fraction - 2.0) / 6.0
    second_node = (fraction + 1.0) * (fraction - 1.0) * (fraction - 2.0) / 2.0
    third_node = -(fraction + 1.0) * fraction * (fraction - 2.0) / 2.0
    fourth_node = (fraction + 1.0) * fraction * (fraction - 1.0) / 6.0
    zeros = jnp.zeros_like(fraction)
    lower = offsets == -1
    weights = [
        jnp.where(lower, first_node, zeros),
        jnp.where(lower, second_node, first_node),
        jnp.where(lower, third_node, second_node),
        jnp.where(lower, fourth_node, third_node),
        jnp.where(lower, zeros, fourth_node),
    ]
    return jnp.stack(weights, axis=1)


def interpolate(padded, stencil):
    cross, levels, along = (stencil.shape[2], stencil.shape[3], stencil.shape[4])
    summed = jnp.zeros((padded.shape[0], cross, levels, along), jnp.float32)
    for x_step in range(5):
        for l_step in range(5):
            partial_sum = jnp.zeros((padded.shape[0], cross, levels, along), jnp.float32)
            for y_step in range(5):
                partial_sum = (
                    partial_sum
                    + stencil[2, y_step]
                    * padded[
                        :,
                        x_step : x_step + cross,
                        l_step : l_step + levels,
                        y_step : y_step + along,
                    ]
                )
            summed = summed + stencil[0, x_step] * stencil[1, l_step] * partial_sum
    return summed


def coagulate(masses, kernel, coag_target):
    number = jnp.sum(jnp.abs(masses), axis=1)
    losses = jnp.dot(kernel, number, precision=precise, preferred_element_type=jnp.float32)
    bin_index = jnp.arange(BINS, dtype=jnp.int32)
    matches = (coag_target[None, :, :] == bin_index[:, None, None]).astype(jnp.float32)
    redistribute = (matches * kernel[None, :, :]).reshape(BINS * BINS, BINS)
    transfer_rate = jnp.dot(
        redistribute, number, precision=precise, preferred_element_type=jnp.float32
    )
    transfer_rate = transfer_rate.reshape(BINS, BINS, number.shape[1])
    gained = jnp.einsum("bic,ikc->bkc", transfer_rate, masses, precision=precise)
    return (masses + gained) / (1.0 + losses[:, None, :])


def on_device(tracers, courant, shear, offsets, seam_flips, kernel, coag_target):
    gathered_courant, gathered_shear = (
        lax.all_gather(courant, "trc", axis=3, tiled=True),
        lax.all_gather(shear, "trc", axis=3, tiled=True),
    )
    stencil = cubic_taps(fractions(gathered_courant, gathered_shear), offsets)
    tile_index = lax.axis_index("tile")
    tile_count = lax.axis_size("tile")
    left_flag = lax.dynamic_index_in_dim(seam_flips, tile_index, 0, False) == 1
    right_flag = lax.dynamic_index_in_dim(seam_flips, (tile_index + 1) % tile_count, 0, False) == 1

    def widen(tracer_field):
        padded = with_halo(tracer_field, (("tile", 1),), 2)
        left_rim = padded[:, :2]
        right_rim = padded[:, -2:]
        left_rim = jnp.where(left_flag, left_rim[..., ::-1], left_rim)
        right_rim = jnp.where(right_flag, right_rim[..., ::-1], right_rim)
        widened = jnp.concatenate([left_rim, tracer_field, right_rim], axis=1)
        widened = jnp.pad(widened, ((0, 0), (0, 0), (2, 2), (0, 0)), mode="edge")
        return jnp.pad(widened, ((0, 0), (0, 0), (0, 0), (2, 2)), mode="wrap")

    moved_once = interpolate(widen(tracers), stencil)
    padded = widen(moved_once)
    moved_twice = interpolate(padded, stencil)
    cell_field = lax.all_to_all(moved_twice, "trc", split_axis=3, concat_axis=0, tiled=True)
    masses = cell_field.reshape(BINS, COMPS, -1)
    coagulated = coagulate(masses, kernel, coag_target).reshape(cell_field.shape)
    return lax.all_to_all(coagulated, "trc", split_axis=0, concat_axis=3, tiled=True)


def solution(mesh):
    placed = (
        P("trc", "tile", None, None),
        P(None, "tile", None, "trc"),
        P(None, "tile", None, "trc"),
        P(None, "tile", None, None),
        P(),
        P(),
        P(),
    )
    return jax.shard_map(
        on_device,
        mesh=mesh,
        in_specs=placed,
        out_specs=P("trc", "tile", None, None),
        check_vma=False,
    )
```

profile of v0, /device:TPU:0, one launch (start us, length us, event | category | flops | bytes accessed | tf_op | source)
XLA Modules:
  0.0 220.3 jit_solution(6981468215762434635)
XLA Ops:
  0.0 1.2 copy.88
  1.2 3.4 %collective-permute-start.1 = (f32[128,2,2,128]{3,0,2,1:T(8,128)S(1)}, f32[128,2,2,128]{3,0,2,1:T(8,128)S(1)}, u32[]{:S(2)}, u32[]{:S(2)}) collective-permute-start(f32[128,2,2,128]{3,0,2,1:T(8,128)S(1)} %get-tuple-element.47), channel_id=1, source_target_pairs={{4,0},{8,4},{12,8},{16,12},{20,16},{24,20},{28,24},{0,28},{5,1},{9... | collective-permute-start | bytes 786440 | tf_op jit(solution)/shard_map/ppermute | solution.py:23
  4.6 0.8 copy.78
  5.5 14.8 %all_gather.6 = f32[3,4,2,128]{1,2,0,3:T(2,128)S(1)} all-gather(f32[3,4,2,32]{1,2,0,3:T(2,128)S(1)} %copy.78), channel_id=1, replica_groups=mesh['tile'=8,'trc'=4] {'trc'}, dimensions={3}, use_global_device_ids=true | all-gather | bytes 15360 | tf_op jit(solution)/shard_map/all_gather | solution.py:91
  20.3 0.2 copy.85
  20.6 0.8 copy.79
  21.4 15.4 %all_gather.7 = f32[3,4,2,128]{1,2,0,3:T(2,128)S(1)} all-gather(f32[3,4,2,32]{1,2,0,3:T(2,128)S(1)} %copy.79), channel_id=1, replica_groups=mesh['tile'=8,'trc'=4] {'trc'}, dimensions={3}, use_global_device_ids=true | all-gather | bytes 15360 | tf_op jit(solution)/shard_map/all_gather | solution.py:92
  36.8 0.2 copy.84
  37.0 0.1 broadcast_select_fusion.5
  37.2 0.6 fusion.337
  39.4 0.4 rev.13
  39.8 0.0 collective-permute-done
  39.8 0.4 rev.12
  40.3 0.1 pad_maximum_fusion.6
  40.4 0.1 slice_bitcast_fusion.3
  40.5 0.1 reshape.115
  40.6 0.1 reshape.114
  40.7 0.3 pad_maximum_fusion.2
  41.0 1.8 maximum_maximum_fusion.2
  42.8 1.5 fusion.334
  44.4 1.3 fusion.330
  45.7 6.4 %maximum_maximum_fusion = (f32[128,8,6,130]{3,0,2,1:T(8,128)}, f32[128,8,6,130]{3,0,2,1:T(8,128)}) fusion(f32[128,8,2,128]{3,0,2,1:T(8,128)S(1)} %reshape.115, f32[128,2,2,128]{3,0,2,1:T(8,128)S(1)} %broadcast_select_fusion.1, f32[128,4,2,128]{3,0,2,1:T(8,128)S(1)} %copy.88, f32[128,2,2,128]{3,0,2,1:T(8,128)S(1)} %broadcast_select_fusion.3, ...), kind=kLoop, calls=%fused_computation | loop fusion | flops 7987200 | bytes 9633792 | tf_op jit(solution)/shard_map/jit(_pad)/concatenate | solution.py:108
  52.1 36.1 %fusion.49 = f32[128,4,2,128]{3,0,2,1:T(8,128)S(1)} fusion(f32[128,4,2,128]{3,0,2,1:T(8,128)S(1)} %copy.88, f32[128,2,2,128]{3,0,2,1:T(8,128)S(1)} %broadcast_select_fusion.1, f32[128,2,2,128]{3,0,2,1:T(8,128)} %copy-done, f32[128,8,6,130]{3,0,2,1:T(8,128)} %get-tuple-element.13, f32[128,8,6,130]{3,0,2,1:T(8,128)} %get-tuple-element.12, ...), kind=kLoop, calls=%fused_computation.70 | loop fusion | flops 36438016 | bytes 61988864 | tf_op jit(solution)/shard_map/add | solution.py:71
  88.2 0.1 collective-permute-start.3
  88.3 0.5 collective-permute-start.2
  88.8 6.0 %collective-permute-done.3 = f32[128,2,2,128]{3,0,2,1:T(8,128)S(1)} collective-permute-done((f32[128,2,2,128]{3,0,2,1:T(8,128)S(1)}, f32[128,2,2,128]{3,0,2,1:T(8,128)S(1)}, u32[]{:S(2)}, u32[]{:S(2)}) %collective-permute-start.3) | collective-permute-done | bytes 262176 | tf_op jit(solution)/shard_map/ppermute | solution.py:23
  94.8 0.3 rev.15
  95.2 1.3 collective-permute-done.2
  96.4 0.3 rev.14
  96.8 0.1 pad_maximum_fusion.7
  96.9 0.1 slice_bitcast_fusion.1
  97.0 0.1 reshape.127
  97.1 0.1 reshape.126
  97.2 0.3 pad_maximum_fusion.3
  97.5 1.8 maximum_maximum_fusion.3
  99.4 1.1 fusion.332
  100.4 1.1 fusion.331
  101.5 1.3 fusion.329
  102.8 6.4 %maximum_maximum_fusion.1 = (f32[128,8,6,130]{3,0,2,1:T(8,128)}, f32[128,8,6,130]{3,0,2,1:T(8,128)}) fusion(f32[128,8,2,128]{3,0,2,1:T(8,128)S(1)} %reshape.127, f32[128,2,2,128]{3,0,2,1:T(8,128)S(1)} %broadcast_select_fusion, f32[128,4,2,128]{3,0,2,1:T(8,128)S(1)} %fusion.49, f32[128,2,2,128]{3,0,2,1:T(8,128)S(1)} %broadcast_select_fusion.2, ...), kind=kLoop, calls=%fused_computation.2 | loop fusion | flops 7987200 | bytes 9633792 | tf_op jit(solution)/shard_map/jit(_pad)/concatenate | solution.py:108
  109.2 38.6 %fusion.14 = f32[128,4,2,128]{3,0,2,1:T(8,128)} fusion(f32[128,4,2,128]{3,0,2,1:T(8,128)S(1)} %fusion.49, f32[128,2,2,128]{3,0,2,1:T(8,128)S(1)} %broadcast_select_fusion, f32[128,2,2,128]{3,0,2,1:T(8,128)S(1)} %broadcast_select_fusion.2, f32[128,8,6,130]{3,0,2,1:T(8,128)} %get-tuple-element.9, f32[128,8,6,130]{3,0,2,1:T(8,128)} %get-tuple-element.8, ...), kind=kLoop, calls=%fused_computation.35 | loop fusion | flops 36438016 | bytes 61988864 | tf_op jit(solution)/shard_map/add | solution.py:71
  147.9 1.4 copy.122
  149.3 18.6 %all_to_all.33 = f32[128,4,2,128]{0,2,1,3:T(2,128)S(1)} all-to-all(f32[128,4,2,128]{0,2,1,3:T(2,128)S(1)} %copy.122), channel_id=1, replica_groups=mesh['tile'=8,'trc'=4] {'trc'}, dimensions={3} | all-to-all | bytes 1048576 | tf_op jit(solution)/shard_map/all_to_all | solution.py:113
  167.9 0.1 copy.123
  168.0 1.5 copy.124
  169.5 0.0 copy-start.1
  169.5 0.0 copy-start.2
  169.5 2.3 %reshape.138 = f32[32,16,256]{2,1,0:T(8,128)S(1)} reshape(f32[4,128,4,2,32]{4,3,2,1,0:T(2,128)S(1)} %copy.124) | data formatting | bytes 1048576 | tf_op jit(solution)/shard_map/reshape | solution.py:114
  171.8 1.4 copy.125
  173.3 0.1 abs_reduce_fusion
  173.4 0.2 fusion
  173.6 1.9 fusion.312
  175.5 5.3 %copy.126 = f32[32,32,256]{1,0,2:T(8,128)} copy(f32[32,32,256]{2,1,0:T(8,128)} %fusion.312) | data formatting | bytes 2097152 | tf_op jit(solution)/shard_map/dot_general | solution.py:81
  180.9 9.3 %fusion.338 = f32[256,16,32]{2,1,0:T(8,128)} fusion(f32[32,16,256]{0,1,2:T(8,128)S(1)} %copy.125, f32[32,32,256]{1,0,2:T(8,128)} %copy.126), kind=kOutput, calls=%fused_computation.632 | convolution fusion | flops 50331648 | bytes 2097152 | tf_op jit(solution)/shard_map/bic,ikc->bkc/dot_general | solution.py:85
  190.2 2.7 %copy.127 = f32[256,16,32]{0,1,2:T(8,128)S(1)} copy(f32[256,16,32]{2,1,0:T(8,128)} %fusion.338) | data formatting | bytes 1048576 | tf_op jit(solution)/shard_map/bic,ikc->bkc/dot_general | solution.py:85
  192.9 0.1 fusion.311
  193.0 1.7 reshape.139
  194.7 2.5 %reshape.161 = f32[4,1,32768]{2,1,0:T(1,128)S(1)} reshape(f32[512,4,2,32]{3,2,1,0:T(2,128)S(1)} %reshape.139) | data formatting | bytes 1048576
  197.2 16.0 %all_to_all.34 = f32[4,1,32768]{2,1,0:T(1,128)S(1)} all-to-all(f32[4,1,32768]{2,1,0:T(1,128)S(1)} %reshape.161), channel_id=1, replica_groups=mesh['tile'=8,'trc'=4] {'trc'}, dimensions={0} | all-to-all | bytes 1048576 | tf_op jit(solution)/shard_map/all_to_all | solution.py:116
  213.2 0.5 broadcast.159
  213.7 2.1 reduce
  215.9 1.8 reshape.162
  217.7 1.5 copy.131
  219.2 0.1 copy.129
  219.3 1.0 copy.130
  (50 shorter events, 0.4 us)
Async XLA Ops:
  0.0 37.0 %copy-start.3 = (s32[3,4,2,128]{3,2,1,0:T(2,128)S(1)}, s32[3,4,2,128]{3,2,1,0:T(2,128)}, u32[]{:S(2)}) copy-start(s32[3,4,2,128]{3,2,1,0:T(2,128)} %param.10) | copy-start | bytes 36868
  0.0 37.1 %copy-start.4 = (s32[8]{0:T(128)S(1)}, s32[8]{0:T(128)}, u32[]{:S(2)}) copy-start(s32[8]{0:T(128)} %param.11) | copy-start | bytes 100
  1.2 38.2 %collective-permute-start.1 = (f32[128,2,2,128]{3,0,2,1:T(8,128)S(1)}, f32[128,2,2,128]{3,0,2,1:T(8,128)S(1)}, u32[]{:S(2)}, u32[]{:S(2)}) collective-permute-start(f32[128,2,2,128]{3,0,2,1:T(8,128)S(1)} %get-tuple-element.47), channel_id=1, source_target_pairs={{4,0},{8,4},{12,8},{16,12},{20,16},{24,20},{28,24},{0,28},{5,1},{9... | collective-permute-start | bytes 786440 | tf_op jit(solution)/shard_map/ppermute | solution.py:23
  4.6 35.2 %collective-permute-start = (f32[128,2,2,128]{3,0,2,1:T(8,128)S(1)}, f32[128,2,2,128]{3,0,2,1:T(8,128)S(1)}, u32[]{:S(2)}, u32[]{:S(2)}) collective-permute-start(f32[128,2,2,128]{3,0,2,1:T(8,128)S(1)} %get-tuple-element.46), channel_id=1, source_target_pairs={{0,4},{4,8},{8,12},{12,16},{16,20},{20,24},{24,28},{28,0},{1,5},{5... | collective-permute-start | bytes 786440 | tf_op jit(solution)/shard_map/ppermute | solution.py:21
  40.3 5.4 %copy-start = (f32[128,2,2,128]{3,0,2,1:T(8,128)}, f32[128,2,2,128]{3,0,2,1:T(8,128)S(1)}, u32[]{:S(2)}) copy-start(f32[128,2,2,128]{3,0,2,1:T(8,128)S(1)} %broadcast_select_fusion.3) | copy-start | bytes 786436
  88.2 6.6 %collective-permute-start.3 = (f32[128,2,2,128]{3,0,2,1:T(8,128)S(1)}, f32[128,2,2,128]{3,0,2,1:T(8,128)S(1)}, u32[]{:S(2)}, u32[]{:S(2)}) collective-permute-start(f32[128,2,2,128]{3,0,2,1:T(8,128)S(1)} %get-tuple-element.35), channel_id=1, source_target_pairs={{4,0},{8,4},{12,8},{16,12},{20,16},{24,20},{28,24},{0,28},{5,1},{9... | collective-permute-start | bytes 786440 | tf_op jit(solution)/shard_map/ppermute | solution.py:23
  88.3 8.2 %collective-permute-start.2 = (f32[128,2,2,128]{3,0,2,1:T(8,128)S(1)}, f32[128,2,2,128]{3,0,2,1:T(8,128)S(1)}, u32[]{:S(2)}, u32[]{:S(2)}) collective-permute-start(f32[128,2,2,128]{3,0,2,1:T(8,128)S(1)} %get-tuple-element.34), channel_id=1, source_target_pairs={{0,4},{4,8},{8,12},{12,16},{16,20},{20,24},{24,28},{28,0},{1,5},{5... | collective-permute-start | bytes 786440 | tf_op jit(solution)/shard_map/ppermute | solution.py:21
  169.5 3.9 %copy-start.1 = (f32[32,32]{1,0:T(8,128)S(1)}, f32[32,32]{1,0:T(8,128)}, u32[]{:S(2)}) copy-start(f32[32,32]{1,0:T(8,128)} %param.12) | copy-start | bytes 12292
  169.5 4.1 %copy-start.2 = (s32[32,32]{1,0:T(8,128)S(1)}, s32[32,32]{1,0:T(8,128)}, u32[]{:S(2)}) copy-start(s32[32,32]{1,0:T(8,128)} %param.13) | copy-start | bytes 12292
where the time goes:
time: 221 us; the launch traced here: 220 us
  other arithmetic  94.6 us (43%)
  blocking collectives  64.9 us (29%)
  local copies, waits for them, and re-layouts  36.2 us (16%)
  matrix products  11.4 us (5%)
  waiting for transfers between devices  7.28 us (3%)
  starting transfers between devices  3.97 us (2%)
    add x2, other arithmetic, interpolate(): summed = summed + stencil[0, x_step] * stencil[1, l_step] * partial_sum  74.7 us
    all_to_all x1, blocking collectives, on_device(): lax.all_to_all(moved_twice, 'trc', split_axis=3, concat_axis=0, tiled=True)  18.6 us
    all_to_all x1, blocking collectives, on_device(): lax.all_to_all(coagulated, 'trc', split_axis=0, concat_axis=3, tiled=True)  16 us
    all_gather x1, blocking collectives, on_device(): lax.all_gather(shear, 'trc', axis=3, tiled=True)  15.4 us
    all_gather x1, blocking collectives, on_device(): lax.all_gather(courant, 'trc', axis=3, tiled=True)  14.8 us
    concatenate x2, other arithmetic, widen(): return jnp.pad(widened, ((0, 0), (0, 0), (0, 0), (2, 2)), mode='wrap')  12.8 us
    dot_general x1, matrix products, coagulate(): jnp.einsum('bic,ikc->bkc', transfer_rate, masses, precision=precise)  9.31 us
    unnamed x15, local copies, waits for them, and re-layouts  7.16 us
  transfers between devices with their start and end apart: 4, of which 2 were waited for; matrix products, arithmetic and copies ran while one was open for 2% of the time, Pallas kernels for 0%

commit v1 on v0

v1 whole, which is shorter than its diff:
```python
import functools

import jax
import jax.numpy as jnp
from jax import lax
from jax.experimental import pallas as pl
from jax.experimental.pallas import tpu as pltpu
from jax.sharding import PartitionSpec as P

BINS = 32
COMPS = 16
ITER = 3
REACH = 2
SUB = 8
VMEM = pltpu.VMEM
SMEM = pltpu.SMEM


def shift(value, axis, step):
    count = lax.axis_size(axis)
    return lax.ppermute(value, axis, [(i, (i + step) % count) for i in range(count)])


def fractions(courant, shear):
    fraction = jnp.full(courant.shape, 0.5, jnp.float32)
    for _ in range(ITER):
        fraction = jax.nn.sigmoid(courant + shear * (fraction - 0.5))
    return fraction


def taps_of(fraction, lower):
    nodes = [
        -fraction * (fraction - 1.0) * (fraction - 2.0) / 6.0,
        (fraction + 1.0) * (fraction - 1.0) * (fraction - 2.0) / 2.0,
        -(fraction + 1.0) * fraction * (fraction - 2.0) / 2.0,
        (fraction + 1.0) * fraction * (fraction - 1.0) / 6.0,
    ]
    zeros = jnp.zeros_like(fraction)
    below = nodes + [zeros]
    above = [zeros] + nodes
    return [jnp.where(lower, p, q) for p, q in zip(below, above)]


def reversed_if(flag, value):
    lanes = value.shape[1]
    lane = lax.broadcasted_iota(jnp.int32, (SUB, lanes), 1)
    index = jnp.where(flag, lanes - 1 - lane, lane)
    return jnp.take_along_axis(value, index, axis=1)


def transport_kernel(dims, flips_ref, small_ref, own_ref, left_ref, right_ref, *rest):
    cross, levels, along, groups, parts = dims
    rows = cross * levels
    edge = REACH * levels
    wide = rows + 2 * edge
    outs = rest[:-4]
    weights, raw, once, final = rest[-4:]
    tile = lax.axis_index("tile")
    tiles = lax.axis_size("tile")
    spot = lax.axis_index("trc")
    flip_left = flips_ref[tile] == 1
    flip_right = flips_ref[lax.rem(tile + 1, tiles)] == 1
    chunk = along // lax.axis_size("trc")

    small = pltpu.roll(small_ref[...], (spot + 1) * chunk, 1)
    pieces = [small[k : k + SUB] for k in range(0, small.shape[0], SUB)]
    left_turn = jnp.concatenate([reversed_if(flip_left, p) for p in pieces], axis=0)
    right_turn = jnp.concatenate([reversed_if(flip_right, p) for p in pieces], axis=0)
    row = lax.broadcasted_iota(jnp.int32, (wide, along), 0)
    in_left = row < edge
    in_right = row >= wide - edge
    turned = (in_left & flip_left) | (in_right & flip_right)
    level = lax.rem(row, levels)

    def piece(k):
        part = slice(k * wide, (k + 1) * wide)
        return jnp.where(in_left, left_turn[part], jnp.where(in_right, right_turn[part], small[part]))

    taps = [taps_of(piece(d), piece(3 + d) < -0.5) for d in range(3)]
    count = 2 * REACH + 1
    for b in range(count):
        weights[b] = jnp.where(turned, taps[2][count - 1 - b], taps[2][b])
    for l in range(levels):
        share = jnp.zeros((wide, along), jnp.float32)
        for c in range(count):
            source = jnp.clip(level + (c - REACH), 0, levels - 1)
            share = share + jnp.where(source == l, taps[1][c], 0.0)
        for a in range(count):
            weights[count + a * levels + l] = taps[0][a] * share

    def spread(store, at, value):
        for b in range(count):
            back = (REACH - b) % along
            store[b, at] = value if back == 0 else pltpu.roll(value, back, 1)

    def combine(store, first, at):
        totals = [None] * levels
        for a in range(count):
            for l in range(levels):
                values = [store[b, (first + a) * levels + l] for b in range(count)]
                for o in range(levels):
                    r = at + o
                    inner = weights[0, r : r + 1] * values[0]
                    for b in range(1, count):
                        inner = inner + weights[b, r : r + 1] * values[b]
                    k = count + a * levels + l
                    term = weights[k, r : r + 1] * inner
                    totals[o] = term if totals[o] is None else totals[o] + term
        return totals

    def group(i, carry):
        base = i * (SUB * rows)
        for side, (ref, flag) in enumerate(((left_ref, flip_left), (own_ref, None), (right_ref, flip_right))):
            for j in range(rows):
                value = ref[pl.ds(base + j, SUB, rows), :]
                if flag is not None:
                    value = reversed_if(flag, value)
                spread(raw, side * rows + j, value)
        for x in range(cross + 2 * REACH):
            for l, value in enumerate(combine(raw, x + cross - 2 * REACH, x * levels)):
                spread(once, x * levels + l, value)
        for x in range(cross):
            for l, value in enumerate(combine(once, x, (x + REACH) * levels)):
                final[x * levels + l, pl.ds(pl.multiple_of(i * SUB, SUB), SUB), :] = value
        return carry

    lax.fori_loop(0, groups, group, 0)
    if len(outs) == 1:
        outs[0][...] = final[...]
    else:
        each = rows // parts
        for s in range(parts):
            start = lax.rem(spot + s, parts) * each
            outs[s][...] = final[pl.ds(start, each)]


def transported(small, own, left, right, flips, cross, levels, parts):
    tracers = own.shape[0] // (cross * levels)
    along = own.shape[1]
    rows = cross * levels
    wide = rows + 2 * REACH * levels
    count = 2 * REACH + 1
    split = rows % parts == 0
    shapes = [(rows // parts, tracers, along)] * parts if split else [(rows, tracers, along)]
    dims = (cross, levels, along, tracers // SUB, parts)
    return pl.pallas_call(
        functools.partial(transport_kernel, dims),
        out_shape=[jax.ShapeDtypeStruct(s, jnp.float32) for s in shapes],
        in_specs=[pl.BlockSpec(memory_space=SMEM)] + [pl.BlockSpec(memory_space=VMEM)] * 4,
        out_specs=[pl.BlockSpec(memory_space=VMEM)] * len(shapes),
        scratch_shapes=[
            VMEM((count * (1 + levels), wide, along), jnp.float32),
            VMEM((count, 3 * rows, SUB, along), jnp.float32),
            VMEM((count, wide, SUB, along), jnp.float32),
            VMEM((rows, tracers, along), jnp.float32),
        ],
        name="transport",
    )(flips, small, own, left, right)


def three_way(value):
    first = value.astype(jnp.bfloat16).astype(jnp.float32)
    second = (value - first).astype(jnp.bfloat16).astype(jnp.float32)
    return first, second, value - first - second


def rates_kernel(kernel_ref, target_ref, out_ref):
    k1, k2, k3 = three_way(kernel_ref[...])
    rate = jnp.concatenate([k1, k1, k2, k2, k1, k3], axis=1)
    target = jnp.concatenate([target_ref[...]] * 6, axis=1)
    for b in range(BINS):
        out_ref[pl.ds(b * BINS, BINS), :] = jnp.where(target == b, rate, 0.0).astype(jnp.bfloat16)
    out_ref[pl.ds(BINS * BINS, BINS), :] = rate.astype(jnp.bfloat16)


def rate_table(kernel, target):
    return pl.pallas_call(
        rates_kernel,
        out_shape=jax.ShapeDtypeStruct(((BINS + 1) * BINS, 6 * BINS), jnp.bfloat16),
        in_specs=[pl.BlockSpec(memory_space=VMEM)] * 2,
        out_specs=pl.BlockSpec(memory_space=VMEM),
        name="rates",
    )(kernel, target)


def coagulate_kernel(parts, rates_ref, *rest):
    blocks, outs = rest[:parts], rest[parts : 2 * parts]
    masses, number, transfer, result = rest[2 * parts :]
    spot = lax.axis_index("trc")
    _, each, tracers, lanes = masses.shape
    held = tracers // COMPS
    for s in range(parts):
        masses[lax.rem(spot + parts - s, parts)] = blocks[s][...]

    def mass(r, b, h):
        return masses[b // held, r, pl.ds((b % held) * COMPS + h * SUB, SUB), :]

    halves = COMPS // SUB
    for r in range(each):
        for b in range(BINS):
            total = jnp.abs(mass(r, b, 0))
            for h in range(1, halves):
                total = total + jnp.abs(mass(r, b, h))
            number[pl.ds(b, 1), pl.ds(r * lanes, lanes)] = jnp.sum(total, axis=0, keepdims=True)
    n1, n2, n3 = three_way(number[...])
    stacked = jnp.concatenate([n1, n2, n1, n2, n3, n1], axis=0).astype(jnp.bfloat16)
    transfer[...] = jnp.dot(rates_ref[...], stacked, preferred_element_type=jnp.float32)
    tail = pl.ds(BINS * BINS, BINS)
    transfer[tail, :] = 1.0 / (1.0 + transfer[tail, :])
    block = 4
    for r in range(each):
        lane = pl.ds(r * lanes, lanes)
        for first in range(0, BINS, block):
            bins = range(first, min(first + block, BINS))
            sums = {(b, h): mass(r, b, h) for b in bins for h in range(halves)}
            for i in range(bins[-1] + 1):
                source = [mass(r, i, h) for h in range(halves)]
                for b in bins:
                    if i <= b:
                        rate = transfer[pl.ds(b * BINS + i, 1), lane]
                        for h in range(halves):
                            sums[b, h] = sums[b, h] + rate * source[h]
            for b in bins:
                scale = transfer[pl.ds(BINS * BINS + b, 1), lane]
                for h in range(halves):
                    result[b // held, r, pl.ds((b % held) * COMPS + h * SUB, SUB), :] = sums[b, h] * scale
    for s in range(parts):
        outs[s][...] = result[lax.rem(spot + s, parts)]


def coagulated(rates, blocks):
    parts = len(blocks)
    each, tracers, lanes = blocks[0].shape
    shape = jax.ShapeDtypeStruct(blocks[0].shape, jnp.float32)
    return pl.pallas_call(
        functools.partial(coagulate_kernel, parts),
        out_shape=[shape] * parts,
        in_specs=[pl.BlockSpec(memory_space=VMEM)] * (parts + 1),
        out_specs=[pl.BlockSpec(memory_space=VMEM)] * parts,
        scratch_shapes=[
            VMEM((parts, each, tracers, lanes), jnp.float32),
            VMEM((BINS, each * lanes), jnp.float32),
            VMEM(((BINS + 1) * BINS, each * lanes), jnp.float32),
            VMEM((parts, each, tracers, lanes), jnp.float32),
        ],
        name="coagulate",
    )(rates, *blocks)


def collect_kernel(parts, *rest):
    blocks, out_ref, held = rest[:parts], rest[parts], rest[parts + 1]
    each, tracers, _ = blocks[0].shape
    rows = each * parts
    spot = lax.axis_index("trc")
    for s in range(parts):
        held[pl.ds(lax.rem(spot + parts - s, parts) * each, each)] = blocks[s][...]
    for i in range(tracers // SUB):
        for r in range(rows):
            out_ref[pl.ds(i * SUB * rows + r, SUB, rows), :] = held[r, pl.ds(i * SUB, SUB), :]


def collected(blocks):
    parts = len(blocks)
    each, tracers, along = blocks[0].shape
    rows = each * parts
    return pl.pallas_call(
        functools.partial(collect_kernel, parts),
        out_shape=jax.ShapeDtypeStruct((tracers * rows, along), jnp.float32),
        in_specs=[pl.BlockSpec(memory_space=VMEM)] * parts,
        out_specs=pl.BlockSpec(memory_space=VMEM),
        scratch_shapes=[VMEM((rows, tracers, along), jnp.float32)],
        name="collect",
    )(*blocks)


def on_device(tracers, courant, shear, offsets, seam_flips, kernel, coag_target):
    held, cross, levels, along = tracers.shape
    rows = cross * levels
    parts = lax.axis_size("trc")
    spot = lax.axis_index("trc")
    chunk = along // parts
    edge = REACH * levels

    own_offsets = lax.dynamic_slice_in_dim(offsets, spot * chunk, chunk, 3)
    small = jnp.concatenate([fractions(courant, shear), own_offsets.astype(jnp.float32)], axis=0)
    small = small.reshape(6, rows, chunk)
    below = shift(small[:, rows - edge :], "tile", 1)
    above = shift(small[:, :edge], "tile", -1)
    left = shift(tracers, "tile", 1)
    right = shift(tracers, "tile", -1)
    small = jnp.concatenate([below, small, above], axis=1).reshape(-1, chunk)
    strips = [shift(small, "trc", s) for s in range(parts - 1, 0, -1)] + [small]
    small = jnp.concatenate(strips, axis=1)
    rates = rate_table(kernel, coag_target)

    flat = (held * rows, along)
    blocks = transported(
        small, tracers.reshape(flat), left.reshape(flat), right.reshape(flat), seam_flips, cross, levels, parts
    )
    if len(blocks) == 1:
        lanes = rows * along // parts
        cells = blocks[0].reshape(rows, held, along // lanes, lanes).transpose(0, 2, 1, 3)
        cells = jnp.roll(cells.reshape(parts, 1, held, lanes), -spot, axis=0)
        blocks = [cells[s] for s in range(parts)]
    blocks = [blocks[0]] + [shift(blocks[s], "trc", s) for s in range(1, parts)]
    blocks = coagulated(rates, blocks)
    blocks = [blocks[0]] + [shift(blocks[s], "trc", s) for s in range(1, parts)]
    if rows % parts == 0:
        return collected(blocks).reshape(tracers.shape)
    lanes = blocks[0].shape[-1]
    cells = jnp.stack([blocks[0]] + blocks[:0:-1], axis=0)
    cells = jnp.roll(cells, spot, axis=0).reshape(rows, along // lanes, held, lanes)
    return cells.transpose(2, 0, 1, 3).reshape(tracers.shape)


def solution(mesh):
    placed = (
        P("trc", "tile", None, None),
        P(None, "tile", None, "trc"),
        P(None, "tile", None, "trc"),
        P(None, "tile", None, None),
        P(),
        P(),
        P(),
    )
    return jax.shard_map(
        on_device,
        mesh=mesh,
        in_specs=placed,
        out_specs=P("trc", "tile", None, None),
        check_vma=False,
    )
```

time: 221 us -> 69.5 us (0.31)
  the two profiles are of different devices: /device:TPU:0 before, /device:TPU:11 now
where the time goes in v1:
time: 69.5 us; the launch traced here: 69 us
  waiting for transfers between devices  36.5 us (53%)
  Pallas kernels  16.7 us (24%)
  starting transfers between devices  11.9 us (17%)
  local copies, waits for them, and re-layouts  2.89 us (4%)
  other arithmetic  0.89 us (1%)
    ppermute x13, waiting for transfers between devices, shift(): lax.ppermute(value, axis, [(i, (i + step) % count) for i in range(count)])  36.5 us
    ppermute x13, starting transfers between devices, shift(): lax.ppermute(value, axis, [(i, (i + step) % count) for i in range(count)])  11.9 us
    pallas_call x1, Pallas kernels, transported(): pl.pallas_call(functools.partial(transport_kernel, dims), out_shape=[jax....  9.93 us
    pallas_call x1, Pallas kernels, coagulated(): pl.pallas_call(functools.partial(coagulate_kernel, parts), out_shape=[sha...  3.06 us
    unnamed x22, local copies, waits for them, and re-layouts  2.88 us
    pallas_call x1, Pallas kernels, collected(): pl.pallas_call(functools.partial(collect_kernel, parts), out_shape=jax.Sh...  2.01 us
    pallas_call x1, Pallas kernels, rate_table(): pl.pallas_call(rates_kernel, out_shape=jax.ShapeDtypeStruct(((BINS + 1) *...  1.72 us
  transfers between devices with their start and end apart: 13, of which 9 were waited for; matrix products, arithmetic and copies ran while one was open for 1% of the time, Pallas kernels for 2%

profile of v1, /device:TPU:11, one launch (start us, length us, event | category | flops | bytes accessed | tf_op | source)
XLA Modules:
  0.0 69.0 jit_solution(4886760882984112693)
XLA Ops:
  0.0 0.0 copy-start.8
  0.0 0.7 collective-permute-start.6
  0.7 2.0 %collective-permute-start.5 = (f32[128,4,2,128]{3,2,1,0:T(2,128)}, f32[128,4,2,128]{3,2,1,0:T(2,128)S(1)}, u32[]{:S(2)}, u32[]{:S(2)}) collective-permute-start(f32[128,4,2,128]{3,2,1,0:T(2,128)} %param.7), channel_id=1, source_target_pairs={{0,4},{4,8},{8,12},{12,16},{16,20},{20,24},{24,28},{28,0},{1,5},{5... | collective-permute-start | bytes 1572872 | tf_op jit(solution)/shard_map/ppermute | solution.py:21
  2.6 0.0 copy-done.8
  2.7 0.0 copy-start.9
  2.7 0.0 copy-start.10
  2.7 0.1 dynamic-slice_convert_fusion
  2.7 0.6 copy-done.9
  3.4 0.0 copy-done.10
  3.4 0.1 add_divide_fusion
  3.5 0.1 collective-permute-start
  3.5 0.5 collective-permute-start.1
  4.0 9.0 %collective-permute-done = f32[6,4,32]{2,1,0:T(4,128)S(1)} collective-permute-done((f32[6,4,32]{2,1,0:T(4,128)S(1)}, f32[6,4,32]{2,1,0:T(4,128)S(1)}, u32[]{:S(2)}, u32[]{:S(2)}) %collective-permute-start) | collective-permute-done | bytes 3104 | tf_op jit(solution)/shard_map/ppermute | solution.py:21
  13.1 2.4 %collective-permute-done.1 = f32[6,4,32]{2,1,0:T(4,128)S(1)} collective-permute-done((f32[6,4,32]{2,1,0:T(4,128)S(1)}, f32[6,4,32]{2,1,0:T(4,128)S(1)}, u32[]{:S(2)}, u32[]{:S(2)}) %collective-permute-start.1) | collective-permute-done | bytes 3104 | tf_op jit(solution)/shard_map/ppermute | solution.py:21
  15.5 1.3 %collective-permute-start.4 = (f32[96,32]{1,0:T(8,128)S(1)}, f32[96,32]{1,0:T(8,128)S(1)}, u32[]{:S(2)}, u32[]{:S(2)}) collective-permute-start(f32[96,32]{1,0:T(8,128)S(1)} %bitcast.11), channel_id=1, source_target_pairs={{0,1},{1,2},{2,3},{3,0},{4,5},{5,6},{6,7},{7,4},{8,9},{9,10},{10,1... | collective-permute-start | bytes 36872 | tf_op jit(solution)/shard_map/ppermute | solution.py:21
  16.9 1.1 %collective-permute-start.3 = (f32[96,32]{1,0:T(8,128)S(1)}, f32[96,32]{1,0:T(8,128)S(1)}, u32[]{:S(2)}, u32[]{:S(2)}) collective-permute-start(f32[96,32]{1,0:T(8,128)S(1)} %bitcast.12), channel_id=1, source_target_pairs={{0,2},{1,3},{2,0},{3,1},{4,6},{5,7},{6,4},{7,5},{8,10},{9,11},{10,... | collective-permute-start | bytes 36872 | tf_op jit(solution)/shard_map/ppermute | solution.py:21
  18.0 1.4 %collective-permute-start.2 = (f32[96,32]{1,0:T(8,128)S(1)}, f32[96,32]{1,0:T(8,128)S(1)}, u32[]{:S(2)}, u32[]{:S(2)}) collective-permute-start(f32[96,32]{1,0:T(8,128)S(1)} %bitcast.13), channel_id=1, source_target_pairs={{0,3},{1,0},{2,1},{3,2},{4,7},{5,4},{6,5},{7,6},{8,11},{9,8},{10,9... | collective-permute-start | bytes 36872 | tf_op jit(solution)/shard_map/ppermute | solution.py:21
  19.4 0.0 collective-permute-done.4
  19.4 1.9 %collective-permute-done.3 = f32[96,32]{1,0:T(8,128)S(1)} collective-permute-done((f32[96,32]{1,0:T(8,128)S(1)}, f32[96,32]{1,0:T(8,128)S(1)}, u32[]{:S(2)}, u32[]{:S(2)}) %collective-permute-start.3) | collective-permute-done | bytes 12320 | tf_op jit(solution)/shard_map/ppermute | solution.py:21
  21.2 1.6 %collective-permute-done.2 = f32[96,32]{1,0:T(8,128)S(1)} collective-permute-done((f32[96,32]{1,0:T(8,128)S(1)}, f32[96,32]{1,0:T(8,128)S(1)}, u32[]{:S(2)}, u32[]{:S(2)}) %collective-permute-start.2) | collective-permute-done | bytes 12320 | tf_op jit(solution)/shard_map/ppermute | solution.py:21
  22.8 0.7 %pad_maximum_fusion.1.small_ref = f32[96,128]{1,0:T(8,128)} fusion(f32[96,32]{1,0:T(8,128)S(1)} %bitcast.14, f32[96,32]{1,0:T(8,128)S(1)} %collective-permute-done.4, f32[96,32]{1,0:T(8,128)S(1)} %collective-permute-done.3, f32[96,32]{1,0:T(8,128)S(1)} %collective-permute-done.2), kind=kLoop, calls=%fused_computation.1 | loop fusion | flops 36864 | bytes 98304 | tf_op jit(solution)/shard_map/concatenate | solution.py:293
  23.5 0.0 collective-permute-done.6
  23.5 0.0 copy-start
  23.5 0.0 collective-permute-done.5
  23.5 0.0 copy-start.1
  23.5 0.8 %copy-done = f32[128,4,2,128]{3,2,1,0:T(2,128)} copy-done((f32[128,4,2,128]{3,2,1,0:T(2,128)}, f32[128,4,2,128]{3,2,1,0:T(2,128)S(1)}, u32[]{:S(2)}) %copy-start) | copy-done | bytes 524312
  24.3 0.2 copy-done.1
  24.5 9.9 %transport.1 = (f32[2,128,128]{2,1,0:T(8,128)}, f32[2,128,128]{2,1,0:T(8,128)}, f32[2,128,128]{2,1,0:T(8,128)}, f32[2,128,128]{2,1,0:T(8,128)}) custom-call(s32[8]{0:T(128)} %flips_ref.1, f32[96,128]{1,0:T(8,128)} %pad_maximum_fusion.1.small_ref, f32[1024,128]{1,0:T(8,128)} %bitcast.6, f32[1024,128]{1,0:T(8,128)} %bitcast.8, f32[1024,128]{1,0:T(8,128)} %bitcast.7), custom_call_target="tpu_custom_call" | custom-call | tf_op jit(solution)/shard_map/transport/pallas_call | solution.py:146
  34.4 0.0 collective-permute-start.7
  34.4 2.7 %collective-permute-start.8 = (f32[2,128,128]{2,1,0:T(8,128)}, f32[2,128,128]{2,1,0:T(8,128)S(1)}, u32[]{:S(2)}, u32[]{:S(2)}) collective-permute-start(f32[2,128,128]{2,1,0:T(8,128)} %get-tuple-element.15), channel_id=1, source_target_pairs={{0,2},{1,3},{2,0},{3,1},{4,6},{5,7},{6,4},{7,5},{8,10},{9,11},{10,... | collective-permute-start | bytes 393224 | tf_op jit(solution)/shard_map/ppermute | solution.py:21
  37.2 0.7 collective-permute-start.9
  37.9 1.7 %rates.1.rates_ref = bf16[1056,192]{1,0:T(8,128)(2,1)} custom-call(f32[32,32]{1,0:T(8,128)} %kernel_ref.1, s32[32,32]{1,0:T(8,128)} %target_ref.1), custom_call_target="tpu_custom_call" | custom-call | tf_op jit(solution)/shard_map/rates/pallas_call | solution.py:177
  39.6 0.0 collective-permute-done.7.rest_1_
  39.6 0.0 copy-start.2
  39.6 6.2 %collective-permute-done.8.rest_2_ = f32[2,128,128]{2,1,0:T(8,128)S(1)} collective-permute-done((f32[2,128,128]{2,1,0:T(8,128)}, f32[2,128,128]{2,1,0:T(8,128)S(1)}, u32[]{:S(2)}, u32[]{:S(2)}) %collective-permute-start.8) | collective-permute-done | bytes 131104 | tf_op jit(solution)/shard_map/ppermute | solution.py:21
  45.8 0.0 copy-start.3
  45.8 3.8 %collective-permute-done.9.rest_3_ = f32[2,128,128]{2,1,0:T(8,128)S(1)} collective-permute-done((f32[2,128,128]{2,1,0:T(8,128)}, f32[2,128,128]{2,1,0:T(8,128)S(1)}, u32[]{:S(2)}, u32[]{:S(2)}) %collective-permute-start.9) | collective-permute-done | bytes 131104 | tf_op jit(solution)/shard_map/ppermute | solution.py:21
  49.6 0.0 copy-start.5
  49.6 0.0 copy-done.2
  49.6 0.0 copy-done.3
  49.6 0.6 copy-done.5
  50.2 3.1 %coagulate.1 = (f32[2,128,128]{2,1,0:T(8,128)}, f32[2,128,128]{2,1,0:T(8,128)}, f32[2,128,128]{2,1,0:T(8,128)}, f32[2,128,128]{2,1,0:T(8,128)}) custom-call(bf16[1056,192]{1,0:T(8,128)(2,1)} %rates.1.rates_ref, f32[2,128,128]{2,1,0:T(8,128)} %get-tuple-element.13.rest_0_, f32[2,128,128]{2,1,0:T(8,128)} %copy-done.2, f32[2,128,128]{2,1,0:T(8,128)} %copy-done.3, ...), custom_call_target="tpu_custom_call" | custom-call | tf_op jit(solution)/shard_map/coagulate/pallas_call | solution.py:235
  53.3 0.0 collective-permute-start.10
  53.3 0.5 collective-permute-start.11
  53.8 1.0 %collective-permute-start.12 = (f32[2,128,128]{2,1,0:T(8,128)}, f32[2,128,128]{2,1,0:T(8,128)S(1)}, u32[]{:S(2)}, u32[]{:S(2)}) collective-permute-start(f32[2,128,128]{2,1,0:T(8,128)} %get-tuple-element.20), channel_id=1, source_target_pairs={{0,3},{1,0},{2,1},{3,2},{4,7},{5,4},{6,5},{7,6},{8,11},{9,8},{10,9... | collective-permute-start | bytes 393224 | tf_op jit(solution)/shard_map/ppermute | solution.py:21
  54.7 3.2 %collective-permute-done.10.rest_1_ = f32[2,128,128]{2,1,0:T(8,128)S(1)} collective-permute-done((f32[2,128,128]{2,1,0:T(8,128)}, f32[2,128,128]{2,1,0:T(8,128)S(1)}, u32[]{:S(2)}, u32[]{:S(2)}) %collective-permute-start.10) | collective-permute-done | bytes 131104 | tf_op jit(solution)/shard_map/ppermute | solution.py:21
  57.9 0.0 copy-start.4
  57.9 6.5 %collective-permute-done.11.rest_2_ = f32[2,128,128]{2,1,0:T(8,128)S(1)} collective-permute-done((f32[2,128,128]{2,1,0:T(8,128)}, f32[2,128,128]{2,1,0:T(8,128)S(1)}, u32[]{:S(2)}, u32[]{:S(2)}) %collective-permute-start.11) | collective-permute-done | bytes 131104 | tf_op jit(solution)/shard_map/ppermute | solution.py:21
  64.4 0.0 copy-start.6
  64.4 2.0 %collective-permute-done.12.rest_3_ = f32[2,128,128]{2,1,0:T(8,128)S(1)} collective-permute-done((f32[2,128,128]{2,1,0:T(8,128)}, f32[2,128,128]{2,1,0:T(8,128)S(1)}, u32[]{:S(2)}, u32[]{:S(2)}) %collective-permute-start.12) | collective-permute-done | bytes 131104 | tf_op jit(solution)/shard_map/ppermute | solution.py:21
  66.4 0.0 copy-start.7
  66.4 0.0 copy-done.4
  66.4 0.0 copy-done.6
  66.4 0.6 copy-done.7
  67.0 2.0 %collect.1 = f32[1024,128]{1,0:T(8,128)} custom-call(f32[2,128,128]{2,1,0:T(8,128)} %get-tuple-element.17.rest_0_, f32[2,128,128]{2,1,0:T(8,128)} %copy-done.4, f32[2,128,128]{2,1,0:T(8,128)} %copy-done.6, f32[2,128,128]{2,1,0:T(8,128)} %copy-done.7), custom_call_target="tpu_custom_call" | custom-call | tf_op jit(solution)/shard_map/collect/pallas_call | solution.py:266
  (3 shorter events, 0.0 us)
Async XLA Ops:
  0.0 2.6 %copy-start.8 = (s32[3,4,2,128]{3,2,1,0:T(2,128)S(1)}, s32[3,4,2,128]{3,2,1,0:T(2,128)}, u32[]{:S(2)}) copy-start(s32[3,4,2,128]{3,2,1,0:T(2,128)} %param.10) | copy-start | bytes 36868
  0.0 23.5 %collective-permute-start.6 = (f32[128,4,2,128]{3,2,1,0:T(2,128)}, f32[128,4,2,128]{3,2,1,0:T(2,128)S(1)}, u32[]{:S(2)}, u32[]{:S(2)}) collective-permute-start(f32[128,4,2,128]{3,2,1,0:T(2,128)} %param.7), channel_id=1, source_target_pairs={{0,28},{4,0},{8,4},{12,8},{16,12},{20,16},{24,20},{28,24},{1,29},{... | collective-permute-start | bytes 1572872 | tf_op jit(solution)/shard_map/ppermute | solution.py:21
  0.7 22.9 %collective-permute-start.5 = (f32[128,4,2,128]{3,2,1,0:T(2,128)}, f32[128,4,2,128]{3,2,1,0:T(2,128)S(1)}, u32[]{:S(2)}, u32[]{:S(2)}) collective-permute-start(f32[128,4,2,128]{3,2,1,0:T(2,128)} %param.7), channel_id=1, source_target_pairs={{0,4},{4,8},{8,12},{12,16},{16,20},{20,24},{24,28},{28,0},{1,5},{5... | collective-permute-start | bytes 1572872 | tf_op jit(solution)/shard_map/ppermute | solution.py:21
  2.7 0.7 %copy-start.9 = (f32[3,4,2,32]{3,2,1,0:T(2,128)S(1)}, f32[3,4,2,32]{3,2,1,0:T(2,128)}, u32[]{:S(2)}) copy-start(f32[3,4,2,32]{3,2,1,0:T(2,128)} %param.8) | copy-start | bytes 9220
  2.7 0.7 %copy-start.10 = (f32[3,4,2,32]{3,2,1,0:T(2,128)S(1)}, f32[3,4,2,32]{3,2,1,0:T(2,128)}, u32[]{:S(2)}) copy-start(f32[3,4,2,32]{3,2,1,0:T(2,128)} %param.9) | copy-start | bytes 9220
  3.5 9.6 %collective-permute-start = (f32[6,4,32]{2,1,0:T(4,128)S(1)}, f32[6,4,32]{2,1,0:T(4,128)S(1)}, u32[]{:S(2)}, u32[]{:S(2)}) collective-permute-start(f32[6,4,32]{2,1,0:T(4,128)S(1)} %get-tuple-element.21), channel_id=1, source_target_pairs={{0,4},{4,8},{8,12},{12,16},{16,20},{20,24},{24,28},{28,0},{1,5},{5... | collective-permute-start | bytes 9224 | tf_op jit(solution)/shard_map/ppermute | solution.py:21
  3.5 12.0 %collective-permute-start.1 = (f32[6,4,32]{2,1,0:T(4,128)S(1)}, f32[6,4,32]{2,1,0:T(4,128)S(1)}, u32[]{:S(2)}, u32[]{:S(2)}) collective-permute-start(f32[6,4,32]{2,1,0:T(4,128)S(1)} %get-tuple-element.22), channel_id=1, source_target_pairs={{0,28},{4,0},{8,4},{12,8},{16,12},{20,16},{24,20},{28,24},{1,29},{... | collective-permute-start | bytes 9224 | tf_op jit(solution)/shard_map/ppermute | solution.py:21
  15.5 3.8 %collective-permute-start.4 = (f32[96,32]{1,0:T(8,128)S(1)}, f32[96,32]{1,0:T(8,128)S(1)}, u32[]{:S(2)}, u32[]{:S(2)}) collective-permute-start(f32[96,32]{1,0:T(8,128)S(1)} %bitcast.11), channel_id=1, source_target_pairs={{0,1},{1,2},{2,3},{3,0},{4,5},{5,6},{6,7},{7,4},{8,9},{9,10},{10,1... | collective-permute-start | bytes 36872 | tf_op jit(solution)/shard_map/ppermute | solution.py:21
  16.9 4.4 %collective-permute-start.3 = (f32[96,32]{1,0:T(8,128)S(1)}, f32[96,32]{1,0:T(8,128)S(1)}, u32[]{:S(2)}, u32[]{:S(2)}) collective-permute-start(f32[96,32]{1,0:T(8,128)S(1)} %bitcast.12), channel_id=1, source_target_pairs={{0,2},{1,3},{2,0},{3,1},{4,6},{5,7},{6,4},{7,5},{8,10},{9,11},{10,... | collective-permute-start | bytes 36872 | tf_op jit(solution)/shard_map/ppermute | solution.py:21
  18.0 4.8 %collective-permute-start.2 = (f32[96,32]{1,0:T(8,128)S(1)}, f32[96,32]{1,0:T(8,128)S(1)}, u32[]{:S(2)}, u32[]{:S(2)}) collective-permute-start(f32[96,32]{1,0:T(8,128)S(1)} %bitcast.13), channel_id=1, source_target_pairs={{0,3},{1,0},{2,1},{3,2},{4,7},{5,4},{6,5},{7,6},{8,11},{9,8},{10,9... | collective-permute-start | bytes 36872 | tf_op jit(solution)/shard_map/ppermute | solution.py:21
  23.5 0.8 %copy-start = (f32[128,4,2,128]{3,2,1,0:T(2,128)}, f32[128,4,2,128]{3,2,1,0:T(2,128)S(1)}, u32[]{:S(2)}) copy-start(f32[128,4,2,128]{3,2,1,0:T(2,128)S(1)} %collective-permute-done.6) | copy-start | bytes 1572868
  23.5 1.0 %copy-start.1 = (f32[128,4,2,128]{3,2,1,0:T(2,128)}, f32[128,4,2,128]{3,2,1,0:T(2,128)S(1)}, u32[]{:S(2)}) copy-start(f32[128,4,2,128]{3,2,1,0:T(2,128)S(1)} %collective-permute-done.5) | copy-start | bytes 1572868
  34.4 5.2 %collective-permute-start.7 = (f32[2,128,128]{2,1,0:T(8,128)}, f32[2,128,128]{2,1,0:T(8,128)S(1)}, u32[]{:S(2)}, u32[]{:S(2)}) collective-permute-start(f32[2,128,128]{2,1,0:T(8,128)} %get-tuple-element.14), channel_id=1, source_target_pairs={{0,1},{1,2},{2,3},{3,0},{4,5},{5,6},{6,7},{7,4},{8,9},{9,10},{10,1... | collective-permute-start | bytes 393224 | tf_op jit(solution)/shard_map/ppermute | solution.py:21
  34.4 11.3 %collective-permute-start.8 = (f32[2,128,128]{2,1,0:T(8,128)}, f32[2,128,128]{2,1,0:T(8,128)S(1)}, u32[]{:S(2)}, u32[]{:S(2)}) collective-permute-start(f32[2,128,128]{2,1,0:T(8,128)} %get-tuple-element.15), channel_id=1, source_target_pairs={{0,2},{1,3},{2,0},{3,1},{4,6},{5,7},{6,4},{7,5},{8,10},{9,11},{10,... | collective-permute-start | bytes 393224 | tf_op jit(solution)/shard_map/ppermute | solution.py:21
  37.2 12.4 %collective-permute-start.9 = (f32[2,128,128]{2,1,0:T(8,128)}, f32[2,128,128]{2,1,0:T(8,128)S(1)}, u32[]{:S(2)}, u32[]{:S(2)}) collective-permute-start(f32[2,128,128]{2,1,0:T(8,128)} %get-tuple-element.16), channel_id=1, source_target_pairs={{0,3},{1,0},{2,1},{3,2},{4,7},{5,4},{6,5},{7,6},{8,11},{9,8},{10,9... | collective-permute-start | bytes 393224 | tf_op jit(solution)/shard_map/ppermute | solution.py:21
  39.6 10.0 %copy-start.2 = (f32[2,128,128]{2,1,0:T(8,128)}, f32[2,128,128]{2,1,0:T(8,128)S(1)}, u32[]{:S(2)}) copy-start(f32[2,128,128]{2,1,0:T(8,128)S(1)} %collective-permute-done.7.rest_1_) | copy-start | bytes 393220
  45.8 3.8 %copy-start.3 = (f32[2,128,128]{2,1,0:T(8,128)}, f32[2,128,128]{2,1,0:T(8,128)S(1)}, u32[]{:S(2)}) copy-start(f32[2,128,128]{2,1,0:T(8,128)S(1)} %collective-permute-done.8.rest_2_) | copy-start | bytes 393220
  49.6 0.6 copy-start.5
  53.3 4.7 %collective-permute-start.10 = (f32[2,128,128]{2,1,0:T(8,128)}, f32[2,128,128]{2,1,0:T(8,128)S(1)}, u32[]{:S(2)}, u32[]{:S(2)}) collective-permute-start(f32[2,128,128]{2,1,0:T(8,128)} %get-tuple-element.18), channel_id=1, source_target_pairs={{0,1},{1,2},{2,3},{3,0},{4,5},{5,6},{6,7},{7,4},{8,9},{9,10},{10,1... | collective-permute-start | bytes 393224 | tf_op jit(solution)/shard_map/ppermute | solution.py:21
  53.3 11.1 %collective-permute-start.11 = (f32[2,128,128]{2,1,0:T(8,128)}, f32[2,128,128]{2,1,0:T(8,128)S(1)}, u32[]{:S(2)}, u32[]{:S(2)}) collective-permute-start(f32[2,128,128]{2,1,0:T(8,128)} %get-tuple-element.19), channel_id=1, source_target_pairs={{0,2},{1,3},{2,0},{3,1},{4,6},{5,7},{6,4},{7,5},{8,10},{9,11},{10,... | collective-permute-start | bytes 393224 | tf_op jit(solution)/shard_map/ppermute | solution.py:21
  53.8 12.6 %collective-permute-start.12 = (f32[2,128,128]{2,1,0:T(8,128)}, f32[2,128,128]{2,1,0:T(8,128)S(1)}, u32[]{:S(2)}, u32[]{:S(2)}) collective-permute-start(f32[2,128,128]{2,1,0:T(8,128)} %get-tuple-element.20), channel_id=1, source_target_pairs={{0,3},{1,0},{2,1},{3,2},{4,7},{5,4},{6,5},{7,6},{8,11},{9,8},{10,9... | collective-permute-start | bytes 393224 | tf_op jit(solution)/shard_map/ppermute | solution.py:21
  57.9 8.4 %copy-start.4 = (f32[2,128,128]{2,1,0:T(8,128)}, f32[2,128,128]{2,1,0:T(8,128)S(1)}, u32[]{:S(2)}) copy-start(f32[2,128,128]{2,1,0:T(8,128)S(1)} %collective-permute-done.10.rest_1_) | copy-start | bytes 393220
  64.4 2.0 %copy-start.6 = (f32[2,128,128]{2,1,0:T(8,128)}, f32[2,128,128]{2,1,0:T(8,128)S(1)}, u32[]{:S(2)}) copy-start(f32[2,128,128]{2,1,0:T(8,128)S(1)} %collective-permute-done.11.rest_2_) | copy-start | bytes 393220
  66.4 0.6 copy-start.7

commit v2 on v1

--- a/solution.py
+++ b/solution.py
@@ -7,18 +7,43 @@
 from jax.experimental.pallas import tpu as pltpu
 from jax.sharding import PartitionSpec as P
 
+
 BINS = 32
 COMPS = 16
 ITER = 3
+BATCHES = 2
 REACH = 2
 SUB = 8
 VMEM = pltpu.VMEM
 SMEM = pltpu.SMEM
 
 
+def near(value):
+    return pltpu.with_memory_space_constraint(value, VMEM)
+
+
 def shift(value, axis, step):
     count = lax.axis_size(axis)
     return lax.ppermute(value, axis, [(i, (i + step) % count) for i in range(count)])
+
+
+def doubling(count):
+    return count & (count - 1) == 0
+
+
+def target(spot, step, count):
+    return spot ^ step if doubling(count) else lax.rem(spot + step, count)
+
+
+def source(spot, step, count):
+    return spot ^ step if doubling(count) else lax.rem(spot + count - step, count)
+
+
+def trade(value, axis, step):
+    count = lax.axis_size(axis)
+    if doubling(count):
+        return lax.ppermute(value, axis, [(i, i ^ step) for i in range(count)])
+    return shift(value, axis, step)
 
 
 def fractions(courant, shear):
@@ -41,15 +66,17 @@
     return [jnp.where(lower, p, q) for p, q in zip(below, above)]
 
 
+def lane_of(flag, lanes):
+    lane = lax.broadcasted_iota(jnp.int32, (SUB, lanes), 1)
+    return jnp.where(flag, lanes - 1 - lane, lane)
+
+
 def reversed_if(flag, value):
-    lanes = value.shape[1]
-    lane = lax.broadcasted_iota(jnp.int32, (SUB, lanes), 1)
-    index = jnp.where(flag, lanes - 1 - lane, lane)
-    return jnp.take_along_axis(value, index, axis=1)
+    return jnp.take_along_axis(value, lane_of(flag, value.shape[1]), axis=1)
 
 
 def transport_kernel(dims, flips_ref, small_ref, own_ref, left_ref, right_ref, *rest):
-    cross, levels, along, groups, parts = dims
+    cross, levels, along, groups, parts, skip = dims
     rows = cross * levels
     edge = REACH * levels
     wide = rows + 2 * edge
@@ -60,12 +87,15 @@
     spot = lax.axis_index("trc")
     flip_left = flips_ref[tile] == 1
     flip_right = flips_ref[lax.rem(tile + 1, tiles)] == 1
-    chunk = along // lax.axis_size("trc")
-
-    small = pltpu.roll(small_ref[...], (spot + 1) * chunk, 1)
-    pieces = [small[k : k + SUB] for k in range(0, small.shape[0], SUB)]
-    left_turn = jnp.concatenate([reversed_if(flip_left, p) for p in pieces], axis=0)
-    right_turn = jnp.concatenate([reversed_if(flip_right, p) for p in pieces], axis=0)
+    chunk = along // parts
+
+    def unscrambled(flag):
+        lane = lane_of(flag, along)
+        index = source(spot, lax.div(lane, chunk), parts) * chunk + lax.rem(lane, chunk)
+        pieces = [small_ref[k : k + SUB] for k in range(0, small_ref.shape[0], SUB)]
+        return jnp.concatenate([jnp.take_along_axis(p, index, axis=1) for p in pieces], axis=0)
+
+    small, left_turn, right_turn = unscrambled(False), unscrambled(flip_left), unscrambled(flip_right)
     row = lax.broadcasted_iota(jnp.int32, (wide, along), 0)
     in_left = row < edge
     in_right = row >= wide - edge
@@ -83,8 +113,8 @@
     for l in range(levels):
         share = jnp.zeros((wide, along), jnp.float32)
         for c in range(count):
-            source = jnp.clip(level + (c - REACH), 0, levels - 1)
-            share = share + jnp.where(source == l, taps[1][c], 0.0)
+            read = jnp.clip(level + (c - REACH), 0, levels - 1)
+            share = share + jnp.where(read == l, taps[1][c], 0.0)
         for a in range(count):
             weights[count + a * levels + l] = taps[0][a] * share
 
@@ -112,7 +142,7 @@
         base = i * (SUB * rows)
         for side, (ref, flag) in enumerate(((left_ref, flip_left), (own_ref, None), (right_ref, flip_right))):
             for j in range(rows):
-                value = ref[pl.ds(base + j, SUB, rows), :]
+                value = ref[pl.ds(base + (skip * rows if side == 1 else 0) + j, SUB, rows), :]
                 if flag is not None:
                     value = reversed_if(flag, value)
                 spread(raw, side * rows + j, value)
@@ -130,22 +160,22 @@
     else:
         each = rows // parts
         for s in range(parts):
-            start = lax.rem(spot + s, parts) * each
+            start = target(spot, s, parts) * each
             outs[s][...] = final[pl.ds(start, each)]
 
 
-def transported(small, own, left, right, flips, cross, levels, parts):
-    tracers = own.shape[0] // (cross * levels)
+def transported(small, own, left, right, flips, cross, levels, parts, skip):
+    tracers = left.shape[0] // (cross * levels)
     along = own.shape[1]
     rows = cross * levels
     wide = rows + 2 * REACH * levels
     count = 2 * REACH + 1
     split = rows % parts == 0
     shapes = [(rows // parts, tracers, along)] * parts if split else [(rows, tracers, along)]
-    dims = (cross, levels, along, tracers // SUB, parts)
+    dims = (cross, levels, along, tracers // SUB, parts, skip)
     return pl.pallas_call(
         functools.partial(transport_kernel, dims),
-        out_shape=[jax.ShapeDtypeStruct(s, jnp.float32) for s in shapes],
+        out_shape=[VMEM(s, jnp.float32) for s in shapes],
         in_specs=[pl.BlockSpec(memory_space=SMEM)] + [pl.BlockSpec(memory_space=VMEM)] * 4,
         out_specs=[pl.BlockSpec(memory_space=VMEM)] * len(shapes),
         scratch_shapes=[
@@ -155,7 +185,7 @@
             VMEM((rows, tracers, along), jnp.float32),
         ],
         name="transport",
-    )(flips, small, own, left, right)
+    )(flips, *map(near, (small, own, left, right)))
 
 
 def three_way(value):
@@ -176,7 +206,7 @@
 def rate_table(kernel, target):
     return pl.pallas_call(
         rates_kernel,
-        out_shape=jax.ShapeDtypeStruct(((BINS + 1) * BINS, 6 * BINS), jnp.bfloat16),
+        out_shape=VMEM(((BINS + 1) * BINS, 6 * BINS), jnp.bfloat16),
         in_specs=[pl.BlockSpec(memory_space=VMEM)] * 2,
         out_specs=pl.BlockSpec(memory_space=VMEM),
         name="rates",
@@ -184,13 +214,14 @@
 
 
 def coagulate_kernel(parts, rates_ref, *rest):
-    blocks, outs = rest[:parts], rest[parts : 2 * parts]
-    masses, number, transfer, result = rest[2 * parts :]
+    masses, number, transfer, result = rest[-4:]
+    blocks, outs = rest[: -4 - parts], rest[-4 - parts : -4]
     spot = lax.axis_index("trc")
     _, each, tracers, lanes = masses.shape
     held = tracers // COMPS
-    for s in range(parts):
-        masses[lax.rem(spot + parts - s, parts)] = blocks[s][...]
+    for at, block in enumerate(blocks):
+        size = block.shape[1]
+        masses[source(spot, at % parts, parts), :, pl.ds(at // parts * size, size)] = block[...]
 
     def mass(r, b, h):
         return masses[b // held, r, pl.ds((b % held) * COMPS + h * SUB, SUB), :]
@@ -214,28 +245,27 @@
             bins = range(first, min(first + block, BINS))
             sums = {(b, h): mass(r, b, h) for b in bins for h in range(halves)}
             for i in range(bins[-1] + 1):
-                source = [mass(r, i, h) for h in range(halves)]
+                inner = [mass(r, i, h) for h in range(halves)]
                 for b in bins:
                     if i <= b:
                         rate = transfer[pl.ds(b * BINS + i, 1), lane]
                         for h in range(halves):
-                            sums[b, h] = sums[b, h] + rate * source[h]
+                            sums[b, h] = sums[b, h] + rate * inner[h]
             for b in bins:
                 scale = transfer[pl.ds(BINS * BINS + b, 1), lane]
                 for h in range(halves):
                     result[b // held, r, pl.ds((b % held) * COMPS + h * SUB, SUB), :] = sums[b, h] * scale
     for s in range(parts):
-        outs[s][...] = result[lax.rem(spot + s, parts)]
-
-
-def coagulated(rates, blocks):
-    parts = len(blocks)
-    each, tracers, lanes = blocks[0].shape
-    shape = jax.ShapeDtypeStruct(blocks[0].shape, jnp.float32)
+        outs[s][...] = result[target(spot, s, parts)]
+
+
+def coagulated(rates, blocks, parts):
+    each, size, lanes = blocks[0].shape
+    tracers = size * (len(blocks) // parts)
     return pl.pallas_call(
         functools.partial(coagulate_kernel, parts),
-        out_shape=[shape] * parts,
-        in_specs=[pl.BlockSpec(memory_space=VMEM)] * (parts + 1),
+        out_shape=[VMEM((each, tracers, lanes), jnp.float32)] * parts,
+        in_specs=[pl.BlockSpec(memory_space=VMEM)] * (len(blocks) + 1),
         out_specs=[pl.BlockSpec(memory_space=VMEM)] * parts,
         scratch_shapes=[
             VMEM((parts, each, tracers, lanes), jnp.float32),
@@ -244,7 +274,7 @@
             VMEM((parts, each, tracers, lanes), jnp.float32),
         ],
         name="coagulate",
-    )(rates, *blocks)
+    )(*map(near, (rates, *blocks)))
 
 
 def collect_kernel(parts, *rest):
@@ -253,7 +283,7 @@
     rows = each * parts
     spot = lax.axis_index("trc")
     for s in range(parts):
-        held[pl.ds(lax.rem(spot + parts - s, parts) * each, each)] = blocks[s][...]
+        held[pl.ds(source(spot, s, parts) * each, each)] = blocks[s][...]
     for i in range(tracers // SUB):
         for r in range(rows):
             out_ref[pl.ds(i * SUB * rows + r, SUB, rows), :] = held[r, pl.ds(i * SUB, SUB), :]
@@ -270,7 +300,7 @@
         out_specs=pl.BlockSpec(memory_space=VMEM),
         scratch_shapes=[VMEM((rows, tracers, along), jnp.float32)],
         name="collect",
-    )(*blocks)
+    )(*map(near, blocks))
 
 
 def on_device(tracers, courant, shear, offsets, seam_flips, kernel, coag_target):
@@ -280,36 +310,51 @@
     spot = lax.axis_index("trc")
     chunk = along // parts
     edge = REACH * levels
+    batches = BATCHES if held % (BATCHES * SUB) == 0 else 1
+    size = held // batches
 
     own_offsets = lax.dynamic_slice_in_dim(offsets, spot * chunk, chunk, 3)
     small = jnp.concatenate([fractions(courant, shear), own_offsets.astype(jnp.float32)], axis=0)
     small = small.reshape(6, rows, chunk)
     below = shift(small[:, rows - edge :], "tile", 1)
     above = shift(small[:, :edge], "tile", -1)
-    left = shift(tracers, "tile", 1)
-    right = shift(tracers, "tile", -1)
+    left, right = [], []
+    for k in range(batches):
+        batch = tracers[k * size : (k + 1) * size]
+        left.append(shift(batch, "tile", 1))
+        right.append(shift(batch, "tile", -1))
     small = jnp.concatenate([below, small, above], axis=1).reshape(-1, chunk)
-    strips = [shift(small, "trc", s) for s in range(parts - 1, 0, -1)] + [small]
+    strips = [small]
+    for s in range(1, parts):
+        strips.append(trade(small, "trc", s))
     small = jnp.concatenate(strips, axis=1)
     rates = rate_table(kernel, coag_target)
 
-    flat = (held * rows, along)
-    blocks = transported(
-        small, tracers.reshape(flat), left.reshape(flat), right.reshape(flat), seam_flips, cross, levels, parts
-    )
-    if len(blocks) == 1:
-        lanes = rows * along // parts
-        cells = blocks[0].reshape(rows, held, along // lanes, lanes).transpose(0, 2, 1, 3)
-        cells = jnp.roll(cells.reshape(parts, 1, held, lanes), -spot, axis=0)
-        blocks = [cells[s] for s in range(parts)]
-    blocks = [blocks[0]] + [shift(blocks[s], "trc", s) for s in range(1, parts)]
-    blocks = coagulated(rates, blocks)
-    blocks = [blocks[0]] + [shift(blocks[s], "trc", s) for s in range(1, parts)]
+    flat = (-1, along)
+    own = tracers.reshape(flat)
+    gathered = []
+    for k in range(batches):
+        blocks = transported(
+            small, own, left[k].reshape(flat), right[k].reshape(flat), seam_flips, cross, levels, parts, k * size
+        )
+        if len(blocks) == 1:
+            lanes = rows * along // parts
+            cells = blocks[0].reshape(rows, size, along // lanes, lanes).transpose(0, 2, 1, 3)
+            cells = cells.reshape(parts, 1, size, lanes)
+            blocks = [lax.dynamic_index_in_dim(cells, target(spot, s, parts), 0, False) for s in range(parts)]
+        gathered.append(blocks[0])
+        for s in range(1, parts):
+            gathered.append(trade(blocks[s], "trc", s))
+    blocks = coagulated(rates, gathered, parts)
+    returned = [blocks[0]]
+    for s in range(1, parts):
+        returned.append(trade(blocks[s], "trc", s))
     if rows % parts == 0:
-        return collected(blocks).reshape(tracers.shape)
+        return collected(returned).reshape(tracers.shape)
     lanes = blocks[0].shape[-1]
-    cells = jnp.stack([blocks[0]] + blocks[:0:-1], axis=0)
-    cells = jnp.roll(cells, spot, axis=0).reshape(rows, along // lanes, held, lanes)
+    cells = jnp.stack(returned, axis=0)
+    cells = cells[jnp.stack([source(spot, jnp.int32(c), parts) if doubling(parts) else lax.rem(spot - c + parts, parts) for c in range(parts)])]
+    cells = cells.reshape(rows, along // lanes, held, lanes)
     return cells.transpose(2, 0, 1, 3).reshape(tracers.shape)
 
 
@@ -323,6 +368,7 @@
         P(),
         P(),
     )
+
     return jax.shard_map(
         on_device,
         mesh=mesh,

time: 69.5 us -> 60.3 us (0.87)
  the two profiles are of different devices: /device:TPU:11 before, /device:TPU:0 now
where the time goes in v2:
time: 60.3 us; the launch traced here: 59.8 us
  starting transfers between devices  26.1 us (43%)
  waiting for transfers between devices  18.9 us (31%)
  Pallas kernels  12 us (20%)
  local copies, waits for them, and re-layouts  2.42 us (4%)
    ppermute x12, starting transfers between devices, trade(): return lax.ppermute(value, axis, [(i, i ^ step) for i in range(count)])  19.2 us
    ppermute x12, waiting for transfers between devices, trade(): return lax.ppermute(value, axis, [(i, i ^ step) for i in range(count)])  18.9 us
    pallas_call x2, Pallas kernels, transported(): pl.pallas_call(functools.partial(transport_kernel, dims), out_shape=[VMEM...  9.15 us
    ppermute x6, starting transfers between devices, shift(): lax.ppermute(value, axis, [(i, (i + step) % count) for i in range(count)])  6.86 us
    unnamed x8, local copies, waits for them, and re-layouts  1.35 us
  transfers between devices with their start and end apart: 18, of which 7 were waited for; matrix products, arithmetic and copies ran while one was open for 2% of the time, Pallas kernels for 17%

profile of v2, /device:TPU:0, one launch (start us, length us, event | category | flops | bytes accessed | tf_op | source)
XLA Modules:
  0.0 59.8 jit_solution(3180859622514118625)
XLA Ops:
  0.0 0.0 copy-start.1
  0.0 0.7 %copy-done.1 = s32[3,4,2,128]{3,2,1,0:T(2,128)S(1)} copy-done((s32[3,4,2,128]{3,2,1,0:T(2,128)S(1)}, s32[3,4,2,128]{3,2,1,0:T(2,128)}, u32[]{:S(2)}) %copy-start.1) | copy-done | bytes 12312
  0.7 0.0 copy-start.2
  0.7 0.0 copy-start.3
  0.7 0.1 dynamic-slice_convert_fusion
  0.8 0.6 %copy-done.2 = f32[3,4,2,32]{3,2,1,0:T(2,128)S(1)} copy-done((f32[3,4,2,32]{3,2,1,0:T(2,128)S(1)}, f32[3,4,2,32]{3,2,1,0:T(2,128)}, u32[]{:S(2)}) %copy-start.2) | copy-done | bytes 3096
  1.4 0.0 copy-done.3
  1.4 0.1 add_divide_fusion
  1.5 0.5 collective-permute-start
  2.1 0.0 copy-start
  2.1 2.9 %collective-permute-start.1 = (f32[6,4,32]{2,1,0:T(4,128)S(1)}, f32[6,4,32]{2,1,0:T(4,128)S(1)}, u32[]{:S(2)}, u32[]{:S(2)}) collective-permute-start(f32[6,4,32]{2,1,0:T(4,128)S(1)} %get-tuple-element.32), channel_id=1, source_target_pairs={{0,28},{4,0},{8,4},{12,8},{16,12},{20,16},{24,20},{28,24},{1,29},{... | collective-permute-start | bytes 9224 | tf_op jit(solution)/shard_map/ppermute | solution.py:27
  5.0 1.1 %fusion = (f32[64,4,2,128]{3,2,1,0:T(2,128)S(1)}, f32[64,4,2,128]{3,2,1,0:T(2,128)S(1)}) fusion(f32[128,4,2,128]{3,2,1,0:T(2,128)} %param.7), kind=kLoop, calls=%fused_computation.5 | loop fusion | bytes 1048576 | tf_op jit(solution)/shard_map/slice | solution.py:323
  6.1 0.7 %collective-permute-start.11 = (f32[64,4,2,128]{3,2,1,0:T(2,128)S(1)}, f32[64,4,2,128]{3,2,1,0:T(2,128)S(1)}, u32[]{:S(2)}, u32[]{:S(2)}) collective-permute-start(f32[64,4,2,128]{3,2,1,0:T(2,128)S(1)} %get-tuple-element.29), channel_id=1, source_target_pairs={{0,28},{4,0},{8,4},{12,8},{16,12},{20,16},{24,20},{28,24},{1,29},{... | collective-permute-start | bytes 786440 | tf_op jit(solution)/shard_map/ppermute | solution.py:27
  6.8 0.0 collective-permute-start.10
  6.8 2.6 %collective-permute-start.6 = (f32[64,4,2,128]{3,2,1,0:T(2,128)S(1)}, f32[64,4,2,128]{3,2,1,0:T(2,128)S(1)}, u32[]{:S(2)}, u32[]{:S(2)}) collective-permute-start(f32[64,4,2,128]{3,2,1,0:T(2,128)S(1)} %get-tuple-element.30), channel_id=1, source_target_pairs={{0,28},{4,0},{8,4},{12,8},{16,12},{20,16},{24,20},{28,24},{1,29},{... | collective-permute-start | bytes 786440 | tf_op jit(solution)/shard_map/ppermute | solution.py:27
  9.5 0.0 collective-permute-done
  9.5 0.0 collective-permute-start.5
  9.5 0.0 collective-permute-done.1
  9.5 3.7 %collective-permute-start.4 = (f32[96,32]{1,0:T(8,128)S(1)}, f32[96,32]{1,0:T(8,128)S(1)}, u32[]{:S(2)}, u32[]{:S(2)}) collective-permute-start(f32[96,32]{1,0:T(8,128)S(1)} %bitcast.16), channel_id=1, source_target_pairs={{0,3},{1,2},{2,1},{3,0},{4,7},{5,6},{6,5},{7,4},{8,11},{9,10},{10,... | collective-permute-start | bytes 36872 | tf_op jit(solution)/shard_map/ppermute | solution.py:45
  13.2 2.2 %collective-permute-done.4 = f32[96,32]{1,0:T(8,128)S(1)} collective-permute-done((f32[96,32]{1,0:T(8,128)S(1)}, f32[96,32]{1,0:T(8,128)S(1)}, u32[]{:S(2)}, u32[]{:S(2)}) %collective-permute-start.4) | collective-permute-done | bytes 12320 | tf_op jit(solution)/shard_map/ppermute | solution.py:45
  15.5 0.8 %collective-permute-start.3 = (f32[96,32]{1,0:T(8,128)S(1)}, f32[96,32]{1,0:T(8,128)S(1)}, u32[]{:S(2)}, u32[]{:S(2)}) collective-permute-start(f32[96,32]{1,0:T(8,128)S(1)} %bitcast.17), channel_id=1, source_target_pairs={{0,2},{1,3},{2,0},{3,1},{4,6},{5,7},{6,4},{7,5},{8,10},{9,11},{10,... | collective-permute-start | bytes 36872 | tf_op jit(solution)/shard_map/ppermute | solution.py:45
  16.3 4.1 %collective-permute-done.3 = f32[96,32]{1,0:T(8,128)S(1)} collective-permute-done((f32[96,32]{1,0:T(8,128)S(1)}, f32[96,32]{1,0:T(8,128)S(1)}, u32[]{:S(2)}, u32[]{:S(2)}) %collective-permute-start.3) | collective-permute-done | bytes 12320 | tf_op jit(solution)/shard_map/ppermute | solution.py:45
  20.5 1.3 %collective-permute-start.2 = (f32[96,32]{1,0:T(8,128)S(1)}, f32[96,32]{1,0:T(8,128)S(1)}, u32[]{:S(2)}, u32[]{:S(2)}) collective-permute-start(f32[96,32]{1,0:T(8,128)S(1)} %bitcast.18), channel_id=1, source_target_pairs={{0,1},{1,0},{2,3},{3,2},{4,5},{5,4},{6,7},{7,6},{8,9},{9,8},{10,11... | collective-permute-start | bytes 36872 | tf_op jit(solution)/shard_map/ppermute | solution.py:45
  21.8 2.8 %collective-permute-done.2 = f32[96,32]{1,0:T(8,128)S(1)} collective-permute-done((f32[96,32]{1,0:T(8,128)S(1)}, f32[96,32]{1,0:T(8,128)S(1)}, u32[]{:S(2)}, u32[]{:S(2)}) %collective-permute-start.2) | collective-permute-done | bytes 12320 | tf_op jit(solution)/shard_map/ppermute | solution.py:45
  24.6 0.1 pad_maximum_fusion.1.small_ref
  24.7 0.0 collective-permute-done.11
  24.7 0.0 collective-permute-done.10
  24.7 0.0 copy-done
  24.7 4.6 %transport.3 = (f32[2,64,128]{2,1,0:T(8,128)S(1)}, f32[2,64,128]{2,1,0:T(8,128)S(1)}, f32[2,64,128]{2,1,0:T(8,128)S(1)}, f32[2,64,128]{2,1,0:T(8,128)S(1)}) custom-call(s32[8]{0:T(128)} %flips_ref.3, f32[96,128]{1,0:T(8,128)S(1)} %pad_maximum_fusion.1.small_ref, f32[1024,128]{1,0:T(8,128)S(1)} %bitcast.8, f32[512,128]{1,0:T(8,128)S(1)} %bitcast.13, ...), custom_call_target="tpu_custom_call" | custom-call | tf_op jit(solution)/shard_map/transport/pallas_call | solution.py:176
  29.3 1.4 %collective-permute-start.12 = (f32[2,64,128]{2,1,0:T(8,128)S(1)}, f32[2,64,128]{2,1,0:T(8,128)S(1)}, u32[]{:S(2)}, u32[]{:S(2)}) collective-permute-start(f32[2,64,128]{2,1,0:T(8,128)S(1)} %get-tuple-element.22), channel_id=1, source_target_pairs={{0,1},{1,0},{2,3},{3,2},{4,5},{5,4},{6,7},{7,6},{8,9},{9,8},{10,11... | collective-permute-start | bytes 196616 | tf_op jit(solution)/shard_map/ppermute | solution.py:45
  30.6 2.9 %collective-permute-start.13 = (f32[2,64,128]{2,1,0:T(8,128)S(1)}, f32[2,64,128]{2,1,0:T(8,128)S(1)}, u32[]{:S(2)}, u32[]{:S(2)}) collective-permute-start(f32[2,64,128]{2,1,0:T(8,128)S(1)} %get-tuple-element.23), channel_id=1, source_target_pairs={{0,2},{1,3},{2,0},{3,1},{4,6},{5,7},{6,4},{7,5},{8,10},{9,11},{10,... | collective-permute-start | bytes 196616 | tf_op jit(solution)/shard_map/ppermute | solution.py:45
  33.6 0.2 collective-permute-start.14
  33.7 0.0 collective-permute-done.6
  33.7 0.0 collective-permute-done.5
  33.7 4.6 %transport.2 = (f32[2,64,128]{2,1,0:T(8,128)S(1)}, f32[2,64,128]{2,1,0:T(8,128)S(1)}, f32[2,64,128]{2,1,0:T(8,128)S(1)}, f32[2,64,128]{2,1,0:T(8,128)S(1)}) custom-call(s32[8]{0:T(128)} %flips_ref.3, f32[96,128]{1,0:T(8,128)S(1)} %pad_maximum_fusion.1.small_ref, f32[1024,128]{1,0:T(8,128)S(1)} %bitcast.9, f32[512,128]{1,0:T(8,128)S(1)} %bitcast.11, ...), custom_call_target="tpu_custom_call" | custom-call | tf_op jit(solution)/shard_map/transport/pallas_call | solution.py:176
  38.3 0.5 collective-permute-start.7
  38.8 3.8 %collective-permute-start.8 = (f32[2,64,128]{2,1,0:T(8,128)S(1)}, f32[2,64,128]{2,1,0:T(8,128)S(1)}, u32[]{:S(2)}, u32[]{:S(2)}) collective-permute-start(f32[2,64,128]{2,1,0:T(8,128)S(1)} %get-tuple-element.19), channel_id=1, source_target_pairs={{0,2},{1,3},{2,0},{3,1},{4,6},{5,7},{6,4},{7,5},{8,10},{9,11},{10,... | collective-permute-start | bytes 196616 | tf_op jit(solution)/shard_map/ppermute | solution.py:45
  42.6 0.0 collective-permute-done.12.rest_5_
  42.6 0.2 collective-permute-start.9
  42.8 0.9 %rates.1.rates_ref = bf16[1056,192]{1,0:T(8,128)(2,1)S(1)} custom-call(f32[32,32]{1,0:T(8,128)} %kernel_ref.1, s32[32,32]{1,0:T(8,128)} %target_ref.1), custom_call_target="tpu_custom_call" | custom-call | tf_op jit(solution)/shard_map/rates/pallas_call | solution.py:207
  43.7 0.0 collective-permute-done.13.rest_6_
  43.7 0.0 collective-permute-done.14.rest_7_
  43.7 0.0 collective-permute-done.7.rest_1_
  43.7 1.8 %collective-permute-done.8.rest_2_ = f32[2,64,128]{2,1,0:T(8,128)S(1)} collective-permute-done((f32[2,64,128]{2,1,0:T(8,128)S(1)}, f32[2,64,128]{2,1,0:T(8,128)S(1)}, u32[]{:S(2)}, u32[]{:S(2)}) %collective-permute-start.8) | collective-permute-done | bytes 65568 | tf_op jit(solution)/shard_map/ppermute | solution.py:45
  45.6 3.4 %collective-permute-done.9.rest_3_ = f32[2,64,128]{2,1,0:T(8,128)S(1)} collective-permute-done((f32[2,64,128]{2,1,0:T(8,128)S(1)}, f32[2,64,128]{2,1,0:T(8,128)S(1)}, u32[]{:S(2)}, u32[]{:S(2)}) %collective-permute-start.9) | collective-permute-done | bytes 65568 | tf_op jit(solution)/shard_map/ppermute | solution.py:45
  49.0 1.0 %coagulate.1 = (f32[2,128,128]{2,1,0:T(8,128)S(1)}, f32[2,128,128]{2,1,0:T(8,128)S(1)}, f32[2,128,128]{2,1,0:T(8,128)S(1)}, f32[2,128,128]{2,1,0:T(8,128)S(1)}) custom-call(bf16[1056,192]{1,0:T(8,128)(2,1)S(1)} %rates.1.rates_ref, f32[2,64,128]{2,1,0:T(8,128)S(1)} %get-tuple-element.17.rest_0_, f32[2,64,128]{2,1,0:T(8,128)S(1)} %collective-permute-done.7.rest_1_, ...), custom_call_target="tpu_custom_call" | custom-call | tf_op jit(solution)/shard_map/coagulate/pallas_call | solution.py:265
  50.0 0.1 collective-permute-start.15
  50.1 1.2 %collective-permute-start.16 = (f32[2,128,128]{2,1,0:T(8,128)S(1)}, f32[2,128,128]{2,1,0:T(8,128)S(1)}, u32[]{:S(2)}, u32[]{:S(2)}) collective-permute-start(f32[2,128,128]{2,1,0:T(8,128)S(1)} %get-tuple-element.27), channel_id=1, source_target_pairs={{0,2},{1,3},{2,0},{3,1},{4,6},{5,7},{6,4},{7,5},{8,10},{9,11},{10,... | collective-permute-start | bytes 393224 | tf_op jit(solution)/shard_map/ppermute | solution.py:45
  51.3 3.1 %collective-permute-start.17 = (f32[2,128,128]{2,1,0:T(8,128)S(1)}, f32[2,128,128]{2,1,0:T(8,128)S(1)}, u32[]{:S(2)}, u32[]{:S(2)}) collective-permute-start(f32[2,128,128]{2,1,0:T(8,128)S(1)} %get-tuple-element.28), channel_id=1, source_target_pairs={{0,3},{1,2},{2,1},{3,0},{4,7},{5,6},{6,5},{7,4},{8,11},{9,10},{10,... | collective-permute-start | bytes 393224 | tf_op jit(solution)/shard_map/ppermute | solution.py:45
  54.5 2.0 %collective-permute-done.15.rest_1_ = f32[2,128,128]{2,1,0:T(8,128)S(1)} collective-permute-done((f32[2,128,128]{2,1,0:T(8,128)S(1)}, f32[2,128,128]{2,1,0:T(8,128)S(1)}, u32[]{:S(2)}, u32[]{:S(2)}) %collective-permute-start.15) | collective-permute-done | bytes 131104 | tf_op jit(solution)/shard_map/ppermute | solution.py:45
  56.4 0.0 collective-permute-done.16.rest_2_
  56.4 2.5 %collective-permute-done.17.rest_3_ = f32[2,128,128]{2,1,0:T(8,128)S(1)} collective-permute-done((f32[2,128,128]{2,1,0:T(8,128)S(1)}, f32[2,128,128]{2,1,0:T(8,128)S(1)}, u32[]{:S(2)}, u32[]{:S(2)}) %collective-permute-start.17) | collective-permute-done | bytes 131104 | tf_op jit(solution)/shard_map/ppermute | solution.py:45
  58.9 0.9 %collect.1 = f32[1024,128]{1,0:T(8,128)} custom-call(f32[2,128,128]{2,1,0:T(8,128)S(1)} %get-tuple-element.25.rest_0_, f32[2,128,128]{2,1,0:T(8,128)S(1)} %collective-permute-done.15.rest_1_, f32[2,128,128]{2,1,0:T(8,128)S(1)} %collective-permute-done.16.rest_2_, f32[2,128,128]{2,1,0:T(8,128)S(1)} %collective-permute-done.17.rest_3_), custom_call_target="tpu_custom_call" | custom-call | tf_op jit(solution)/shard_map/collect/pallas_call | solution.py:296
  (3 shorter events, 0.0 us)
Async XLA Ops:
  0.0 0.7 %copy-start.1 = (s32[3,4,2,128]{3,2,1,0:T(2,128)S(1)}, s32[3,4,2,128]{3,2,1,0:T(2,128)}, u32[]{:S(2)}) copy-start(s32[3,4,2,128]{3,2,1,0:T(2,128)} %param.10) | copy-start | bytes 36868
  0.7 0.7 %copy-start.2 = (f32[3,4,2,32]{3,2,1,0:T(2,128)S(1)}, f32[3,4,2,32]{3,2,1,0:T(2,128)}, u32[]{:S(2)}) copy-start(f32[3,4,2,32]{3,2,1,0:T(2,128)} %param.8) | copy-start | bytes 9220
  0.7 0.7 %copy-start.3 = (f32[3,4,2,32]{3,2,1,0:T(2,128)S(1)}, f32[3,4,2,32]{3,2,1,0:T(2,128)}, u32[]{:S(2)}) copy-start(f32[3,4,2,32]{3,2,1,0:T(2,128)} %param.9) | copy-start | bytes 9220
  1.5 7.9 %collective-permute-start = (f32[6,4,32]{2,1,0:T(4,128)S(1)}, f32[6,4,32]{2,1,0:T(4,128)S(1)}, u32[]{:S(2)}, u32[]{:S(2)}) collective-permute-start(f32[6,4,32]{2,1,0:T(4,128)S(1)} %get-tuple-element.31), channel_id=1, source_target_pairs={{0,4},{4,8},{8,12},{12,16},{16,20},{20,24},{24,28},{28,0},{1,5},{5... | collective-permute-start | bytes 9224 | tf_op jit(solution)/shard_map/ppermute | solution.py:27
  2.1 22.6 %copy-start = (f32[128,4,2,128]{3,2,1,0:T(2,128)S(1)}, f32[128,4,2,128]{3,2,1,0:T(2,128)}, u32[]{:S(2)}) copy-start(f32[128,4,2,128]{3,2,1,0:T(2,128)} %param.7) | copy-start | bytes 1572868
  2.1 7.4 %collective-permute-start.1 = (f32[6,4,32]{2,1,0:T(4,128)S(1)}, f32[6,4,32]{2,1,0:T(4,128)S(1)}, u32[]{:S(2)}, u32[]{:S(2)}) collective-permute-start(f32[6,4,32]{2,1,0:T(4,128)S(1)} %get-tuple-element.32), channel_id=1, source_target_pairs={{0,28},{4,0},{8,4},{12,8},{16,12},{20,16},{24,20},{28,24},{1,29},{... | collective-permute-start | bytes 9224 | tf_op jit(solution)/shard_map/ppermute | solution.py:27
  6.1 18.6 %collective-permute-start.11 = (f32[64,4,2,128]{3,2,1,0:T(2,128)S(1)}, f32[64,4,2,128]{3,2,1,0:T(2,128)S(1)}, u32[]{:S(2)}, u32[]{:S(2)}) collective-permute-start(f32[64,4,2,128]{3,2,1,0:T(2,128)S(1)} %get-tuple-element.29), channel_id=1, source_target_pairs={{0,28},{4,0},{8,4},{12,8},{16,12},{20,16},{24,20},{28,24},{1,29},{... | collective-permute-start | bytes 786440 | tf_op jit(solution)/shard_map/ppermute | solution.py:27
  6.8 17.9 %collective-permute-start.10 = (f32[64,4,2,128]{3,2,1,0:T(2,128)S(1)}, f32[64,4,2,128]{3,2,1,0:T(2,128)S(1)}, u32[]{:S(2)}, u32[]{:S(2)}) collective-permute-start(f32[64,4,2,128]{3,2,1,0:T(2,128)S(1)} %get-tuple-element.29), channel_id=1, source_target_pairs={{0,4},{4,8},{8,12},{12,16},{16,20},{20,24},{24,28},{28,0},{1,5},{5... | collective-permute-start | bytes 786440 | tf_op jit(solution)/shard_map/ppermute | solution.py:27
  6.8 26.9 %collective-permute-start.6 = (f32[64,4,2,128]{3,2,1,0:T(2,128)S(1)}, f32[64,4,2,128]{3,2,1,0:T(2,128)S(1)}, u32[]{:S(2)}, u32[]{:S(2)}) collective-permute-start(f32[64,4,2,128]{3,2,1,0:T(2,128)S(1)} %get-tuple-element.30), channel_id=1, source_target_pairs={{0,28},{4,0},{8,4},{12,8},{16,12},{20,16},{24,20},{28,24},{1,29},{... | collective-permute-start | bytes 786440 | tf_op jit(solution)/shard_map/ppermute | solution.py:27
  9.5 24.3 %collective-permute-start.5 = (f32[64,4,2,128]{3,2,1,0:T(2,128)S(1)}, f32[64,4,2,128]{3,2,1,0:T(2,128)S(1)}, u32[]{:S(2)}, u32[]{:S(2)}) collective-permute-start(f32[64,4,2,128]{3,2,1,0:T(2,128)S(1)} %get-tuple-element.30), channel_id=1, source_target_pairs={{0,4},{4,8},{8,12},{12,16},{16,20},{20,24},{24,28},{28,0},{1,5},{5... | collective-permute-start | bytes 786440 | tf_op jit(solution)/shard_map/ppermute | solution.py:27
  9.5 6.0 %collective-permute-start.4 = (f32[96,32]{1,0:T(8,128)S(1)}, f32[96,32]{1,0:T(8,128)S(1)}, u32[]{:S(2)}, u32[]{:S(2)}) collective-permute-start(f32[96,32]{1,0:T(8,128)S(1)} %bitcast.16), channel_id=1, source_target_pairs={{0,3},{1,2},{2,1},{3,0},{4,7},{5,6},{6,5},{7,4},{8,11},{9,10},{10,... | collective-permute-start | bytes 36872 | tf_op jit(solution)/shard_map/ppermute | solution.py:45
  15.5 5.0 %collective-permute-start.3 = (f32[96,32]{1,0:T(8,128)S(1)}, f32[96,32]{1,0:T(8,128)S(1)}, u32[]{:S(2)}, u32[]{:S(2)}) collective-permute-start(f32[96,32]{1,0:T(8,128)S(1)} %bitcast.17), channel_id=1, source_target_pairs={{0,2},{1,3},{2,0},{3,1},{4,6},{5,7},{6,4},{7,5},{8,10},{9,11},{10,... | collective-permute-start | bytes 36872 | tf_op jit(solution)/shard_map/ppermute | solution.py:45
  20.5 4.1 %collective-permute-start.2 = (f32[96,32]{1,0:T(8,128)S(1)}, f32[96,32]{1,0:T(8,128)S(1)}, u32[]{:S(2)}, u32[]{:S(2)}) collective-permute-start(f32[96,32]{1,0:T(8,128)S(1)} %bitcast.18), channel_id=1, source_target_pairs={{0,1},{1,0},{2,3},{3,2},{4,5},{5,4},{6,7},{7,6},{8,9},{9,8},{10,11... | collective-permute-start | bytes 36872 | tf_op jit(solution)/shard_map/ppermute | solution.py:45
  29.3 13.3 %collective-permute-start.12 = (f32[2,64,128]{2,1,0:T(8,128)S(1)}, f32[2,64,128]{2,1,0:T(8,128)S(1)}, u32[]{:S(2)}, u32[]{:S(2)}) collective-permute-start(f32[2,64,128]{2,1,0:T(8,128)S(1)} %get-tuple-element.22), channel_id=1, source_target_pairs={{0,1},{1,0},{2,3},{3,2},{4,5},{5,4},{6,7},{7,6},{8,9},{9,8},{10,11... | collective-permute-start | bytes 196616 | tf_op jit(solution)/shard_map/ppermute | solution.py:45
  30.6 13.1 %collective-permute-start.13 = (f32[2,64,128]{2,1,0:T(8,128)S(1)}, f32[2,64,128]{2,1,0:T(8,128)S(1)}, u32[]{:S(2)}, u32[]{:S(2)}) collective-permute-start(f32[2,64,128]{2,1,0:T(8,128)S(1)} %get-tuple-element.23), channel_id=1, source_target_pairs={{0,2},{1,3},{2,0},{3,1},{4,6},{5,7},{6,4},{7,5},{8,10},{9,11},{10,... | collective-permute-start | bytes 196616 | tf_op jit(solution)/shard_map/ppermute | solution.py:45
  33.6 10.2 %collective-permute-start.14 = (f32[2,64,128]{2,1,0:T(8,128)S(1)}, f32[2,64,128]{2,1,0:T(8,128)S(1)}, u32[]{:S(2)}, u32[]{:S(2)}) collective-permute-start(f32[2,64,128]{2,1,0:T(8,128)S(1)} %get-tuple-element.24), channel_id=1, source_target_pairs={{0,3},{1,2},{2,1},{3,0},{4,7},{5,6},{6,5},{7,4},{8,11},{9,10},{10,... | collective-permute-start | bytes 196616 | tf_op jit(solution)/shard_map/ppermute | solution.py:45
  38.3 5.4 %collective-permute-start.7 = (f32[2,64,128]{2,1,0:T(8,128)S(1)}, f32[2,64,128]{2,1,0:T(8,128)S(1)}, u32[]{:S(2)}, u32[]{:S(2)}) collective-permute-start(f32[2,64,128]{2,1,0:T(8,128)S(1)} %get-tuple-element.18), channel_id=1, source_target_pairs={{0,1},{1,0},{2,3},{3,2},{4,5},{5,4},{6,7},{7,6},{8,9},{9,8},{10,11... | collective-permute-start | bytes 196616 | tf_op jit(solution)/shard_map/ppermute | solution.py:45
  38.8 6.8 %collective-permute-start.8 = (f32[2,64,128]{2,1,0:T(8,128)S(1)}, f32[2,64,128]{2,1,0:T(8,128)S(1)}, u32[]{:S(2)}, u32[]{:S(2)}) collective-permute-start(f32[2,64,128]{2,1,0:T(8,128)S(1)} %get-tuple-element.19), channel_id=1, source_target_pairs={{0,2},{1,3},{2,0},{3,1},{4,6},{5,7},{6,4},{7,5},{8,10},{9,11},{10,... | collective-permute-start | bytes 196616 | tf_op jit(solution)/shard_map/ppermute | solution.py:45
  42.6 6.4 %collective-permute-start.9 = (f32[2,64,128]{2,1,0:T(8,128)S(1)}, f32[2,64,128]{2,1,0:T(8,128)S(1)}, u32[]{:S(2)}, u32[]{:S(2)}) collective-permute-start(f32[2,64,128]{2,1,0:T(8,128)S(1)} %get-tuple-element.20), channel_id=1, source_target_pairs={{0,3},{1,2},{2,1},{3,0},{4,7},{5,6},{6,5},{7,4},{8,11},{9,10},{10,... | collective-permute-start | bytes 196616 | tf_op jit(solution)/shard_map/ppermute | solution.py:45
  50.0 6.4 %collective-permute-start.15 = (f32[2,128,128]{2,1,0:T(8,128)S(1)}, f32[2,128,128]{2,1,0:T(8,128)S(1)}, u32[]{:S(2)}, u32[]{:S(2)}) collective-permute-start(f32[2,128,128]{2,1,0:T(8,128)S(1)} %get-tuple-element.26), channel_id=1, source_target_pairs={{0,1},{1,0},{2,3},{3,2},{4,5},{5,4},{6,7},{7,6},{8,9},{9,8},{10,11... | collective-permute-start | bytes 393224 | tf_op jit(solution)/shard_map/ppermute | solution.py:45
  50.1 6.4 %collective-permute-start.16 = (f32[2,128,128]{2,1,0:T(8,128)S(1)}, f32[2,128,128]{2,1,0:T(8,128)S(1)}, u32[]{:S(2)}, u32[]{:S(2)}) collective-permute-start(f32[2,128,128]{2,1,0:T(8,128)S(1)} %get-tuple-element.27), channel_id=1, source_target_pairs={{0,2},{1,3},{2,0},{3,1},{4,6},{5,7},{6,4},{7,5},{8,10},{9,11},{10,... | collective-permute-start | bytes 393224 | tf_op jit(solution)/shard_map/ppermute | solution.py:45
  51.3 7.6 %collective-permute-start.17 = (f32[2,128,128]{2,1,0:T(8,128)S(1)}, f32[2,128,128]{2,1,0:T(8,128)S(1)}, u32[]{:S(2)}, u32[]{:S(2)}) collective-permute-start(f32[2,128,128]{2,1,0:T(8,128)S(1)} %get-tuple-element.28), channel_id=1, source_target_pairs={{0,3},{1,2},{2,1},{3,0},{4,7},{5,6},{6,5},{7,4},{8,11},{9,10},{10,... | collective-permute-start | bytes 393224 | tf_op jit(solution)/shard_map/ppermute | solution.py:45

commit v3 on v2

--- a/solution.py
+++ b/solution.py
@@ -15,7 +15,6 @@
 REACH = 2
 SUB = 8
 VMEM = pltpu.VMEM
-SMEM = pltpu.SMEM
 
 
 def near(value):
@@ -75,18 +74,11 @@
     return jnp.take_along_axis(value, lane_of(flag, value.shape[1]), axis=1)
 
 
-def transport_kernel(dims, flips_ref, small_ref, own_ref, left_ref, right_ref, *rest):
-    cross, levels, along, groups, parts, skip = dims
-    rows = cross * levels
+def fill_weights(dims, flip_left, flip_right, small_ref, weights):
+    cross, levels, along, _, parts, _ = dims
     edge = REACH * levels
-    wide = rows + 2 * edge
-    outs = rest[:-4]
-    weights, raw, once, final = rest[-4:]
-    tile = lax.axis_index("tile")
-    tiles = lax.axis_size("tile")
-    spot = lax.axis_index("trc")
-    flip_left = flips_ref[tile] == 1
-    flip_right = flips_ref[lax.rem(tile + 1, tiles)] == 1
+    wide = cross * levels + 2 * edge
+    spot = lax.axis_index("trc")
     chunk = along // parts
 
     def unscrambled(flag):
@@ -99,7 +91,8 @@
     row = lax.broadcasted_iota(jnp.int32, (wide, along), 0)
     in_left = row < edge
     in_right = row >= wide - edge
-    turned = (in_left & flip_left) | (in_right & flip_right)
+    whole = [jnp.concatenate([f] * (wide // SUB), axis=0) for f in (flip_left, flip_right)]
+    turned = (in_left & whole[0]) | (in_right & whole[1])
     level = lax.rem(row, levels)
 
     def piece(k):
@@ -117,6 +110,21 @@
             share = share + jnp.where(read == l, taps[1][c], 0.0)
         for a in range(count):
             weights[count + a * levels + l] = taps[0][a] * share
+
+
+def transport_kernel(dims, first, flips_ref, small_ref, own_ref, left_ref, right_ref, *rest):
+    cross, levels, along, groups, parts, skip = dims
+    rows = cross * levels
+    *outs, raw, once, final = rest
+    spot = lax.axis_index("trc")
+    flip_left = flips_ref[0:SUB] == 1
+    flip_right = flips_ref[SUB : 2 * SUB] == 1
+    count = 2 * REACH + 1
+    if first:
+        weights, *outs = outs
+        fill_weights(dims, flip_left, flip_right, small_ref, weights)
+    else:
+        weights = small_ref
 
     def spread(store, at, value):
         for b in range(count):
@@ -164,28 +172,30 @@
             outs[s][...] = final[pl.ds(start, each)]
 
 
-def transported(small, own, left, right, flips, cross, levels, parts, skip):
+def transported(stencil, own, left, right, flips, cross, levels, parts, skip):
     tracers = left.shape[0] // (cross * levels)
     along = own.shape[1]
     rows = cross * levels
     wide = rows + 2 * REACH * levels
     count = 2 * REACH + 1
     split = rows % parts == 0
+    first = stencil.ndim == 2
     shapes = [(rows // parts, tracers, along)] * parts if split else [(rows, tracers, along)]
+    kept = [(count * (1 + levels), wide, along)] if first else []
     dims = (cross, levels, along, tracers // SUB, parts, skip)
-    return pl.pallas_call(
-        functools.partial(transport_kernel, dims),
-        out_shape=[VMEM(s, jnp.float32) for s in shapes],
-        in_specs=[pl.BlockSpec(memory_space=SMEM)] + [pl.BlockSpec(memory_space=VMEM)] * 4,
-        out_specs=[pl.BlockSpec(memory_space=VMEM)] * len(shapes),
+    found = pl.pallas_call(
+        functools.partial(transport_kernel, dims, first),
+        out_shape=[VMEM(s, jnp.float32) for s in kept + shapes],
+        in_specs=[pl.BlockSpec(memory_space=VMEM)] * 5,
+        out_specs=[pl.BlockSpec(memory_space=VMEM)] * len(kept + shapes),
         scratch_shapes=[
-            VMEM((count * (1 + levels), wide, along), jnp.float32),
             VMEM((count, 3 * rows, SUB, along), jnp.float32),
             VMEM((count, wide, SUB, along), jnp.float32),
             VMEM((rows, tracers, along), jnp.float32),
         ],
         name="transport",
-    )(flips, *map(near, (small, own, left, right)))
+    )(*map(near, (flips, stencil, own, left, right)))
+    return (found[0], found[1:]) if first else (stencil, found)
 
 
 def three_way(value):
@@ -318,24 +328,32 @@
     small = small.reshape(6, rows, chunk)
     below = shift(small[:, rows - edge :], "tile", 1)
     above = shift(small[:, :edge], "tile", -1)
+    wings = [below, above]
     left, right = [], []
+    early = tracers[:size]
     for k in range(batches):
-        batch = tracers[k * size : (k + 1) * size]
+        if k == 1:
+            wings, late = lax.optimization_barrier((wings, tracers))
+        batch = early if k == 0 else late[k * size : (k + 1) * size]
         left.append(shift(batch, "tile", 1))
         right.append(shift(batch, "tile", -1))
-    small = jnp.concatenate([below, small, above], axis=1).reshape(-1, chunk)
+    small = jnp.concatenate([wings[0], small, wings[1]], axis=1).reshape(-1, chunk)
     strips = [small]
     for s in range(1, parts):
         strips.append(trade(small, "trc", s))
     small = jnp.concatenate(strips, axis=1)
     rates = rate_table(kernel, coag_target)
 
+    tile = lax.axis_index("tile")
+    ends = jnp.stack([tile, lax.rem(tile + 1, lax.axis_size("tile"))])
+    flips = jnp.broadcast_to(jnp.repeat(seam_flips[ends], SUB)[:, None], (2 * SUB, along))
     flat = (-1, along)
+    stencil = small
     own = tracers.reshape(flat)
     gathered = []
     for k in range(batches):
-        blocks = transported(
-            small, own, left[k].reshape(flat), right[k].reshape(flat), seam_flips, cross, levels, parts, k * size
+        stencil, blocks = transported(
+            stencil, own, left[k].reshape(flat), right[k].reshape(flat), flips, cross, levels, parts, k * size
         )
         if len(blocks) == 1:
             lanes = rows * along // parts

time: 60.3 us -> 55.4 us (0.919)
  the two profiles are of different devices: /device:TPU:0 before, /device:TPU:10 now
where the time goes in v3:
time: 55.4 us; the launch traced here: 55.1 us
  waiting for transfers between devices  20.3 us (37%)
  starting transfers between devices  20 us (36%)
  Pallas kernels  11 us (20%)
  local copies, waits for them, and re-layouts  2.57 us (5%)
  other arithmetic  1.09 us (2%)
    ppermute x12, waiting for transfers between devices, trade(): return lax.ppermute(value, axis, [(i, i ^ step) for i in range(count)])  20.3 us
    ppermute x12, starting transfers between devices, trade(): return lax.ppermute(value, axis, [(i, i ^ step) for i in range(count)])  16.2 us
    pallas_call x2, Pallas kernels, transported(): pl.pallas_call(functools.partial(transport_kernel, dims, first), out_shap...  8.18 us
    ppermute x6, starting transfers between devices, shift(): lax.ppermute(value, axis, [(i, (i + step) % count) for i in range(count)])  3.79 us
  transfers between devices with their start and end apart: 18, of which 7 were waited for; matrix products, arithmetic and copies ran while one was open for 4% of the time, Pallas kernels for 17%

profile of v3, /device:TPU:10, one launch (start us, length us, event | category | flops | bytes accessed | tf_op | source)
XLA Modules:
  0.0 55.1 jit_solution(12553099722812968103)
XLA Ops:
  0.0 0.0 copy-start
  0.0 0.0 copy-start.2
  0.0 0.0 copy-start.1
  0.0 0.7 %copy-done.2 = s32[3,4,2,128]{3,2,1,0:T(2,128)S(1)} copy-done((s32[3,4,2,128]{3,2,1,0:T(2,128)S(1)}, s32[3,4,2,128]{3,2,1,0:T(2,128)}, u32[]{:S(2)}) %copy-start.2) | copy-done | bytes 12312
  0.7 0.1 dynamic-slice_convert_fusion
  0.8 0.8 %add_divide_fusion = f32[3,4,2,32]{3,2,1,0:T(2,128)S(1)} fusion(f32[3,4,2,32]{3,2,1,0:T(2,128)} %param.8, f32[3,4,2,32]{3,2,1,0:T(2,128)} %param.9), kind=kLoop, calls=%fused_computation.5 | loop fusion | flops 13056 | bytes 9216 | tf_op jit(solution)/shard_map/div | solution.py:51
  1.6 0.1 collective-permute-start.1
  1.7 0.5 collective-permute-start
  2.2 1.0 %slice.14 = f32[64,4,2,128]{3,2,1,0:T(2,128)S(1)} slice(f32[128,4,2,128]{3,2,1,0:T(2,128)} %param.7), slice={[0:64], [0:4], [0:2], [0:128]} | slice | bytes 524288 | tf_op jit(solution)/shard_map/slice | solution.py:333
  3.2 1.4 %collective-permute-start.6 = (f32[64,4,2,128]{3,2,1,0:T(2,128)S(1)}, f32[64,4,2,128]{3,2,1,0:T(2,128)S(1)}, u32[]{:S(2)}, u32[]{:S(2)}) collective-permute-start(f32[64,4,2,128]{3,2,1,0:T(2,128)S(1)} %slice.14), channel_id=1, source_target_pairs={{0,28},{4,0},{8,4},{12,8},{16,12},{20,16},{24,20},{28,24},{1,29},{... | collective-permute-start | bytes 786440 | tf_op jit(solution)/shard_map/ppermute | solution.py:26
  4.5 0.7 %collective-permute-start.5 = (f32[64,4,2,128]{3,2,1,0:T(2,128)S(1)}, f32[64,4,2,128]{3,2,1,0:T(2,128)S(1)}, u32[]{:S(2)}, u32[]{:S(2)}) collective-permute-start(f32[64,4,2,128]{3,2,1,0:T(2,128)S(1)} %slice.14), channel_id=1, source_target_pairs={{0,4},{4,8},{8,12},{12,16},{16,20},{20,24},{24,28},{28,0},{1,5},{5... | collective-permute-start | bytes 786440 | tf_op jit(solution)/shard_map/ppermute | solution.py:26
  5.3 0.0 collective-permute-done.1
  5.3 0.0 collective-permute-done
  5.3 1.6 %collective-permute-start.4 = (f32[96,32]{1,0:T(8,128)S(1)}, f32[96,32]{1,0:T(8,128)S(1)}, u32[]{:S(2)}, u32[]{:S(2)}) collective-permute-start(f32[96,32]{1,0:T(8,128)S(1)} %bitcast.20), channel_id=1, source_target_pairs={{0,3},{1,2},{2,1},{3,0},{4,7},{5,6},{6,5},{7,4},{8,11},{9,10},{10,... | collective-permute-start | bytes 36872 | tf_op jit(solution)/shard_map/ppermute | solution.py:44
  6.9 1.2 %collective-permute-start.3 = (f32[96,32]{1,0:T(8,128)S(1)}, f32[96,32]{1,0:T(8,128)S(1)}, u32[]{:S(2)}, u32[]{:S(2)}) collective-permute-start(f32[96,32]{1,0:T(8,128)S(1)} %bitcast.21), channel_id=1, source_target_pairs={{0,2},{1,3},{2,0},{3,1},{4,6},{5,7},{6,4},{7,5},{8,10},{9,11},{10,... | collective-permute-start | bytes 36872 | tf_op jit(solution)/shard_map/ppermute | solution.py:44
  8.2 0.1 fusion
  8.2 1.2 %collective-permute-start.2 = (f32[96,32]{1,0:T(8,128)S(1)}, f32[96,32]{1,0:T(8,128)S(1)}, u32[]{:S(2)}, u32[]{:S(2)}) collective-permute-start(f32[96,32]{1,0:T(8,128)S(1)} %bitcast.22), channel_id=1, source_target_pairs={{0,1},{1,0},{2,3},{3,2},{4,5},{5,4},{6,7},{7,6},{8,9},{9,8},{10,11... | collective-permute-start | bytes 36872 | tf_op jit(solution)/shard_map/ppermute | solution.py:44
  9.5 0.0 copy-done.1
  9.5 0.0 collective-permute-done.4
  9.5 0.5 collective-permute-start.11
  10.0 2.4 %collective-permute-done.3 = f32[96,32]{1,0:T(8,128)S(1)} collective-permute-done((f32[96,32]{1,0:T(8,128)S(1)}, f32[96,32]{1,0:T(8,128)S(1)}, u32[]{:S(2)}, u32[]{:S(2)}) %collective-permute-start.3) | collective-permute-done | bytes 12320 | tf_op jit(solution)/shard_map/ppermute | solution.py:44
  12.4 0.6 %collective-permute-start.10 = (f32[64,4,2,128]{3,2,1,0:T(2,128)S(1)}, f32[64,4,2,128]{3,2,1,0:T(2,128)S(1)}, u32[]{:S(2)}, u32[]{:S(2)}) collective-permute-start(f32[64,4,2,128]{3,2,1,0:T(2,128)S(1)} %slice.15), channel_id=1, source_target_pairs={{0,4},{4,8},{8,12},{12,16},{16,20},{20,24},{24,28},{28,0},{1,5},{5... | collective-permute-start | bytes 786440 | tf_op jit(solution)/shard_map/ppermute | solution.py:26
  13.1 0.0 copy-done
  13.1 0.6 %gather_fusion = s32[2]{0:T(128)S(1)} fusion(s32[8]{0:T(128)S(1)} %copy-done, s32[1024]{0:T(1024)S(1)} %pad_clamp_fusion), kind=kCustom, calls=%fused_computation | custom fusion | bytes 24 | tf_op jit(solution)/shard_map/gather | solution.py:349
  13.7 0.1 broadcast_in_dim.11
  13.8 0.1 broadcast_in_dim.12
  13.9 0.0 collective-permute-done.2
  13.9 0.1 pad_maximum_fusion.1.small_ref
  14.0 0.0 collective-permute-done.6
  14.0 0.0 collective-permute-done.5
  14.0 0.1 broadcast_in_dim.13.flips_ref
  14.1 4.2 %transport.2 = (f32[15,16,128]{2,1,0:T(8,128)S(1)}, f32[2,64,128]{2,1,0:T(8,128)S(1)}, f32[2,64,128]{2,1,0:T(8,128)S(1)}, f32[2,64,128]{2,1,0:T(8,128)S(1)}, f32[2,64,128]{2,1,0:T(8,128)S(1)}) custom-call(s32[16,128]{1,0:T(8,128)S(1)} %broadcast_in_dim.13.flips_ref, f32[96,128]{1,0:T(8,128)S(1)} %pad_maximum_fusion.1.small_ref, f32[1024,128]{1,0:T(8,128)S(1)} %bitcast.12, ...), custom_call_target="tpu_custom_call" | custom-call | tf_op jit(solution)/shard_map/transport/pallas_call | solution.py:186
  18.3 2.5 %collective-permute-start.7 = (f32[2,64,128]{2,1,0:T(8,128)S(1)}, f32[2,64,128]{2,1,0:T(8,128)S(1)}, u32[]{:S(2)}, u32[]{:S(2)}) collective-permute-start(f32[2,64,128]{2,1,0:T(8,128)S(1)} %get-tuple-element.24), channel_id=1, source_target_pairs={{0,1},{1,0},{2,3},{3,2},{4,5},{5,4},{6,7},{7,6},{8,9},{9,8},{10,11... | collective-permute-start | bytes 196616 | tf_op jit(solution)/shard_map/ppermute | solution.py:44
  20.9 0.9 %collective-permute-start.8 = (f32[2,64,128]{2,1,0:T(8,128)S(1)}, f32[2,64,128]{2,1,0:T(8,128)S(1)}, u32[]{:S(2)}, u32[]{:S(2)}) collective-permute-start(f32[2,64,128]{2,1,0:T(8,128)S(1)} %get-tuple-element.25), channel_id=1, source_target_pairs={{0,2},{1,3},{2,0},{3,1},{4,6},{5,7},{6,4},{7,5},{8,10},{9,11},{10,... | collective-permute-start | bytes 196616 | tf_op jit(solution)/shard_map/ppermute | solution.py:44
  21.8 0.6 %collective-permute-start.9 = (f32[2,64,128]{2,1,0:T(8,128)S(1)}, f32[2,64,128]{2,1,0:T(8,128)S(1)}, u32[]{:S(2)}, u32[]{:S(2)}) collective-permute-start(f32[2,64,128]{2,1,0:T(8,128)S(1)} %get-tuple-element.26), channel_id=1, source_target_pairs={{0,3},{1,2},{2,1},{3,0},{4,7},{5,6},{6,5},{7,4},{8,11},{9,10},{10,... | collective-permute-start | bytes 196616 | tf_op jit(solution)/shard_map/ppermute | solution.py:44
  22.4 0.0 collective-permute-done.11
  22.4 0.0 collective-permute-done.10
  22.4 4.0 %transport.3 = (f32[2,64,128]{2,1,0:T(8,128)S(1)}, f32[2,64,128]{2,1,0:T(8,128)S(1)}, f32[2,64,128]{2,1,0:T(8,128)S(1)}, f32[2,64,128]{2,1,0:T(8,128)S(1)}) custom-call(s32[16,128]{1,0:T(8,128)S(1)} %broadcast_in_dim.13.flips_ref, f32[15,16,128]{2,1,0:T(8,128)S(1)} %get-tuple-element.27.small_ref, f32[1024,128]{1,0:T(8,128)S(1)} %bitcast.13, ...), custom_call_target="tpu_custom_call" | custom-call | tf_op jit(solution)/shard_map/transport/pallas_call | solution.py:186
  26.4 2.9 %collective-permute-start.12 = (f32[2,64,128]{2,1,0:T(8,128)S(1)}, f32[2,64,128]{2,1,0:T(8,128)S(1)}, u32[]{:S(2)}, u32[]{:S(2)}) collective-permute-start(f32[2,64,128]{2,1,0:T(8,128)S(1)} %get-tuple-element.30), channel_id=1, source_target_pairs={{0,1},{1,0},{2,3},{3,2},{4,5},{5,4},{6,7},{7,6},{8,9},{9,8},{10,11... | collective-permute-start | bytes 196616 | tf_op jit(solution)/shard_map/ppermute | solution.py:44
  29.3 0.7 %collective-permute-start.13 = (f32[2,64,128]{2,1,0:T(8,128)S(1)}, f32[2,64,128]{2,1,0:T(8,128)S(1)}, u32[]{:S(2)}, u32[]{:S(2)}) collective-permute-start(f32[2,64,128]{2,1,0:T(8,128)S(1)} %get-tuple-element.31), channel_id=1, source_target_pairs={{0,2},{1,3},{2,0},{3,1},{4,6},{5,7},{6,4},{7,5},{8,10},{9,11},{10,... | collective-permute-start | bytes 196616 | tf_op jit(solution)/shard_map/ppermute | solution.py:44
  30.0 0.0 collective-permute-done.7.rest_1_
  30.0 0.9 %collective-permute-start.14 = (f32[2,64,128]{2,1,0:T(8,128)S(1)}, f32[2,64,128]{2,1,0:T(8,128)S(1)}, u32[]{:S(2)}, u32[]{:S(2)}) collective-permute-start(f32[2,64,128]{2,1,0:T(8,128)S(1)} %get-tuple-element.32), channel_id=1, source_target_pairs={{0,3},{1,2},{2,1},{3,0},{4,7},{5,6},{6,5},{7,4},{8,11},{9,10},{10,... | collective-permute-start | bytes 196616 | tf_op jit(solution)/shard_map/ppermute | solution.py:44
  30.8 0.9 %rates.1.rates_ref = bf16[1056,192]{1,0:T(8,128)(2,1)S(1)} custom-call(f32[32,32]{1,0:T(8,128)} %kernel_ref.1, s32[32,32]{1,0:T(8,128)} %target_ref.1), custom_call_target="tpu_custom_call" | custom-call | tf_op jit(solution)/shard_map/rates/pallas_call | solution.py:217
  31.8 0.0 collective-permute-done.8.rest_2_
  31.8 0.0 collective-permute-done.9.rest_3_
  31.8 1.1 %collective-permute-done.12.rest_5_ = f32[2,64,128]{2,1,0:T(8,128)S(1)} collective-permute-done((f32[2,64,128]{2,1,0:T(8,128)S(1)}, f32[2,64,128]{2,1,0:T(8,128)S(1)}, u32[]{:S(2)}, u32[]{:S(2)}) %collective-permute-start.12) | collective-permute-done | bytes 65568 | tf_op jit(solution)/shard_map/ppermute | solution.py:44
  32.9 2.0 %collective-permute-done.13.rest_6_ = f32[2,64,128]{2,1,0:T(8,128)S(1)} collective-permute-done((f32[2,64,128]{2,1,0:T(8,128)S(1)}, f32[2,64,128]{2,1,0:T(8,128)S(1)}, u32[]{:S(2)}, u32[]{:S(2)}) %collective-permute-start.13) | collective-permute-done | bytes 65568 | tf_op jit(solution)/shard_map/ppermute | solution.py:44
  34.9 3.1 %collective-permute-done.14.rest_7_ = f32[2,64,128]{2,1,0:T(8,128)S(1)} collective-permute-done((f32[2,64,128]{2,1,0:T(8,128)S(1)}, f32[2,64,128]{2,1,0:T(8,128)S(1)}, u32[]{:S(2)}, u32[]{:S(2)}) %collective-permute-start.14) | collective-permute-done | bytes 65568 | tf_op jit(solution)/shard_map/ppermute | solution.py:44
  38.0 1.0 %coagulate.1 = (f32[2,128,128]{2,1,0:T(8,128)S(1)}, f32[2,128,128]{2,1,0:T(8,128)S(1)}, f32[2,128,128]{2,1,0:T(8,128)S(1)}, f32[2,128,128]{2,1,0:T(8,128)S(1)}) custom-call(bf16[1056,192]{1,0:T(8,128)(2,1)S(1)} %rates.1.rates_ref, f32[2,64,128]{2,1,0:T(8,128)S(1)} %get-tuple-element.23.rest_0_, f32[2,64,128]{2,1,0:T(8,128)S(1)} %collective-permute-done.7.rest_1_, ...), custom_call_target="tpu_custom_call" | custom-call | tf_op jit(solution)/shard_map/coagulate/pallas_call | solution.py:275
  39.0 0.3 collective-permute-start.15
  39.3 2.3 %collective-permute-start.16 = (f32[2,128,128]{2,1,0:T(8,128)S(1)}, f32[2,128,128]{2,1,0:T(8,128)S(1)}, u32[]{:S(2)}, u32[]{:S(2)}) collective-permute-start(f32[2,128,128]{2,1,0:T(8,128)S(1)} %get-tuple-element.35), channel_id=1, source_target_pairs={{0,2},{1,3},{2,0},{3,1},{4,6},{5,7},{6,4},{7,5},{8,10},{9,11},{10,... | collective-permute-start | bytes 393224 | tf_op jit(solution)/shard_map/ppermute | solution.py:44
  41.6 0.9 %collective-permute-start.17 = (f32[2,128,128]{2,1,0:T(8,128)S(1)}, f32[2,128,128]{2,1,0:T(8,128)S(1)}, u32[]{:S(2)}, u32[]{:S(2)}) collective-permute-start(f32[2,128,128]{2,1,0:T(8,128)S(1)} %get-tuple-element.36), channel_id=1, source_target_pairs={{0,3},{1,2},{2,1},{3,0},{4,7},{5,6},{6,5},{7,4},{8,11},{9,10},{10,... | collective-permute-start | bytes 393224 | tf_op jit(solution)/shard_map/ppermute | solution.py:44
  42.5 2.9 %collective-permute-done.15.rest_1_ = f32[2,128,128]{2,1,0:T(8,128)S(1)} collective-permute-done((f32[2,128,128]{2,1,0:T(8,128)S(1)}, f32[2,128,128]{2,1,0:T(8,128)S(1)}, u32[]{:S(2)}, u32[]{:S(2)}) %collective-permute-start.15) | collective-permute-done | bytes 131104 | tf_op jit(solution)/shard_map/ppermute | solution.py:44
  45.4 5.7 %collective-permute-done.16.rest_2_ = f32[2,128,128]{2,1,0:T(8,128)S(1)} collective-permute-done((f32[2,128,128]{2,1,0:T(8,128)S(1)}, f32[2,128,128]{2,1,0:T(8,128)S(1)}, u32[]{:S(2)}, u32[]{:S(2)}) %collective-permute-start.16) | collective-permute-done | bytes 131104 | tf_op jit(solution)/shard_map/ppermute | solution.py:44
  51.1 3.1 %collective-permute-done.17.rest_3_ = f32[2,128,128]{2,1,0:T(8,128)S(1)} collective-permute-done((f32[2,128,128]{2,1,0:T(8,128)S(1)}, f32[2,128,128]{2,1,0:T(8,128)S(1)}, u32[]{:S(2)}, u32[]{:S(2)}) %collective-permute-start.17) | collective-permute-done | bytes 131104 | tf_op jit(solution)/shard_map/ppermute | solution.py:44
  54.2 0.9 %collect.1 = f32[1024,128]{1,0:T(8,128)} custom-call(f32[2,128,128]{2,1,0:T(8,128)S(1)} %get-tuple-element.33.rest_0_, f32[2,128,128]{2,1,0:T(8,128)S(1)} %collective-permute-done.15.rest_1_, f32[2,128,128]{2,1,0:T(8,128)S(1)} %collective-permute-done.16.rest_2_, f32[2,128,128]{2,1,0:T(8,128)S(1)} %collective-permute-done.17.rest_3_), custom_call_target="tpu_custom_call" | custom-call | tf_op jit(solution)/shard_map/collect/pallas_call | solution.py:306
  (5 shorter events, 0.1 us)
Async XLA Ops:
  0.0 13.1 %copy-start = (s32[8]{0:T(128)S(1)}, s32[8]{0:T(128)}, u32[]{:S(2)}) copy-start(s32[8]{0:T(128)} %param.11) | copy-start | bytes 100
  0.0 0.7 %copy-start.2 = (s32[3,4,2,128]{3,2,1,0:T(2,128)S(1)}, s32[3,4,2,128]{3,2,1,0:T(2,128)}, u32[]{:S(2)}) copy-start(s32[3,4,2,128]{3,2,1,0:T(2,128)} %param.10) | copy-start | bytes 36868
  0.0 9.5 %copy-start.1 = (f32[128,4,2,128]{3,2,1,0:T(2,128)S(1)}, f32[128,4,2,128]{3,2,1,0:T(2,128)}, u32[]{:S(2)}) copy-start(f32[128,4,2,128]{3,2,1,0:T(2,128)} %param.7) | copy-start | bytes 1572868
  1.6 3.6 %collective-permute-start.1 = (f32[6,4,32]{2,1,0:T(4,128)S(1)}, f32[6,4,32]{2,1,0:T(4,128)S(1)}, u32[]{:S(2)}, u32[]{:S(2)}) collective-permute-start(f32[6,4,32]{2,1,0:T(4,128)S(1)} %get-tuple-element.37), channel_id=1, source_target_pairs={{0,28},{4,0},{8,4},{12,8},{16,12},{20,16},{24,20},{28,24},{1,29},{... | collective-permute-start | bytes 9224 | tf_op jit(solution)/shard_map/ppermute | solution.py:26
  1.7 3.6 %collective-permute-start = (f32[6,4,32]{2,1,0:T(4,128)S(1)}, f32[6,4,32]{2,1,0:T(4,128)S(1)}, u32[]{:S(2)}, u32[]{:S(2)}) collective-permute-start(f32[6,4,32]{2,1,0:T(4,128)S(1)} %get-tuple-element.38), channel_id=1, source_target_pairs={{0,4},{4,8},{8,12},{12,16},{16,20},{20,24},{24,28},{28,0},{1,5},{5... | collective-permute-start | bytes 9224 | tf_op jit(solution)/shard_map/ppermute | solution.py:26
  3.2 10.8 %collective-permute-start.6 = (f32[64,4,2,128]{3,2,1,0:T(2,128)S(1)}, f32[64,4,2,128]{3,2,1,0:T(2,128)S(1)}, u32[]{:S(2)}, u32[]{:S(2)}) collective-permute-start(f32[64,4,2,128]{3,2,1,0:T(2,128)S(1)} %slice.14), channel_id=1, source_target_pairs={{0,28},{4,0},{8,4},{12,8},{16,12},{20,16},{24,20},{28,24},{1,29},{... | collective-permute-start | bytes 786440 | tf_op jit(solution)/shard_map/ppermute | solution.py:26
  4.5 9.5 %collective-permute-start.5 = (f32[64,4,2,128]{3,2,1,0:T(2,128)S(1)}, f32[64,4,2,128]{3,2,1,0:T(2,128)S(1)}, u32[]{:S(2)}, u32[]{:S(2)}) collective-permute-start(f32[64,4,2,128]{3,2,1,0:T(2,128)S(1)} %slice.14), channel_id=1, source_target_pairs={{0,4},{4,8},{8,12},{12,16},{16,20},{20,24},{24,28},{28,0},{1,5},{5... | collective-permute-start | bytes 786440 | tf_op jit(solution)/shard_map/ppermute | solution.py:26
  5.3 4.2 %collective-permute-start.4 = (f32[96,32]{1,0:T(8,128)S(1)}, f32[96,32]{1,0:T(8,128)S(1)}, u32[]{:S(2)}, u32[]{:S(2)}) collective-permute-start(f32[96,32]{1,0:T(8,128)S(1)} %bitcast.20), channel_id=1, source_target_pairs={{0,3},{1,2},{2,1},{3,0},{4,7},{5,6},{6,5},{7,4},{8,11},{9,10},{10,... | collective-permute-start | bytes 36872 | tf_op jit(solution)/shard_map/ppermute | solution.py:44
  6.9 5.5 %collective-permute-start.3 = (f32[96,32]{1,0:T(8,128)S(1)}, f32[96,32]{1,0:T(8,128)S(1)}, u32[]{:S(2)}, u32[]{:S(2)}) collective-permute-start(f32[96,32]{1,0:T(8,128)S(1)} %bitcast.21), channel_id=1, source_target_pairs={{0,2},{1,3},{2,0},{3,1},{4,6},{5,7},{6,4},{7,5},{8,10},{9,11},{10,... | collective-permute-start | bytes 36872 | tf_op jit(solution)/shard_map/ppermute | solution.py:44
  8.2 5.6 %collective-permute-start.2 = (f32[96,32]{1,0:T(8,128)S(1)}, f32[96,32]{1,0:T(8,128)S(1)}, u32[]{:S(2)}, u32[]{:S(2)}) collective-permute-start(f32[96,32]{1,0:T(8,128)S(1)} %bitcast.22), channel_id=1, source_target_pairs={{0,1},{1,0},{2,3},{3,2},{4,5},{5,4},{6,7},{7,6},{8,9},{9,8},{10,11... | collective-permute-start | bytes 36872 | tf_op jit(solution)/shard_map/ppermute | solution.py:44
  9.5 12.9 %collective-permute-start.11 = (f32[64,4,2,128]{3,2,1,0:T(2,128)S(1)}, f32[64,4,2,128]{3,2,1,0:T(2,128)S(1)}, u32[]{:S(2)}, u32[]{:S(2)}) collective-permute-start(f32[64,4,2,128]{3,2,1,0:T(2,128)S(1)} %slice.15), channel_id=1, source_target_pairs={{0,28},{4,0},{8,4},{12,8},{16,12},{20,16},{24,20},{28,24},{1,29},{... | collective-permute-start | bytes 786440 | tf_op jit(solution)/shard_map/ppermute | solution.py:26
  12.4 10.0 %collective-permute-start.10 = (f32[64,4,2,128]{3,2,1,0:T(2,128)S(1)}, f32[64,4,2,128]{3,2,1,0:T(2,128)S(1)}, u32[]{:S(2)}, u32[]{:S(2)}) collective-permute-start(f32[64,4,2,128]{3,2,1,0:T(2,128)S(1)} %slice.15), channel_id=1, source_target_pairs={{0,4},{4,8},{8,12},{12,16},{16,20},{20,24},{24,28},{28,0},{1,5},{5... | collective-permute-start | bytes 786440 | tf_op jit(solution)/shard_map/ppermute | solution.py:26
  18.3 11.6 %collective-permute-start.7 = (f32[2,64,128]{2,1,0:T(8,128)S(1)}, f32[2,64,128]{2,1,0:T(8,128)S(1)}, u32[]{:S(2)}, u32[]{:S(2)}) collective-permute-start(f32[2,64,128]{2,1,0:T(8,128)S(1)} %get-tuple-element.24), channel_id=1, source_target_pairs={{0,1},{1,0},{2,3},{3,2},{4,5},{5,4},{6,7},{7,6},{8,9},{9,8},{10,11... | collective-permute-start | bytes 196616 | tf_op jit(solution)/shard_map/ppermute | solution.py:44
  20.9 10.9 %collective-permute-start.8 = (f32[2,64,128]{2,1,0:T(8,128)S(1)}, f32[2,64,128]{2,1,0:T(8,128)S(1)}, u32[]{:S(2)}, u32[]{:S(2)}) collective-permute-start(f32[2,64,128]{2,1,0:T(8,128)S(1)} %get-tuple-element.25), channel_id=1, source_target_pairs={{0,2},{1,3},{2,0},{3,1},{4,6},{5,7},{6,4},{7,5},{8,10},{9,11},{10,... | collective-permute-start | bytes 196616 | tf_op jit(solution)/shard_map/ppermute | solution.py:44
  21.8 10.0 %collective-permute-start.9 = (f32[2,64,128]{2,1,0:T(8,128)S(1)}, f32[2,64,128]{2,1,0:T(8,128)S(1)}, u32[]{:S(2)}, u32[]{:S(2)}) collective-permute-start(f32[2,64,128]{2,1,0:T(8,128)S(1)} %get-tuple-element.26), channel_id=1, source_target_pairs={{0,3},{1,2},{2,1},{3,0},{4,7},{5,6},{6,5},{7,4},{8,11},{9,10},{10,... | collective-permute-start | bytes 196616 | tf_op jit(solution)/shard_map/ppermute | solution.py:44
  26.4 6.6 %collective-permute-start.12 = (f32[2,64,128]{2,1,0:T(8,128)S(1)}, f32[2,64,128]{2,1,0:T(8,128)S(1)}, u32[]{:S(2)}, u32[]{:S(2)}) collective-permute-start(f32[2,64,128]{2,1,0:T(8,128)S(1)} %get-tuple-element.30), channel_id=1, source_target_pairs={{0,1},{1,0},{2,3},{3,2},{4,5},{5,4},{6,7},{7,6},{8,9},{9,8},{10,11... | collective-permute-start | bytes 196616 | tf_op jit(solution)/shard_map/ppermute | solution.py:44
  29.3 5.7 %collective-permute-start.13 = (f32[2,64,128]{2,1,0:T(8,128)S(1)}, f32[2,64,128]{2,1,0:T(8,128)S(1)}, u32[]{:S(2)}, u32[]{:S(2)}) collective-permute-start(f32[2,64,128]{2,1,0:T(8,128)S(1)} %get-tuple-element.31), channel_id=1, source_target_pairs={{0,2},{1,3},{2,0},{3,1},{4,6},{5,7},{6,4},{7,5},{8,10},{9,11},{10,... | collective-permute-start | bytes 196616 | tf_op jit(solution)/shard_map/ppermute | solution.py:44
  30.0 8.0 %collective-permute-start.14 = (f32[2,64,128]{2,1,0:T(8,128)S(1)}, f32[2,64,128]{2,1,0:T(8,128)S(1)}, u32[]{:S(2)}, u32[]{:S(2)}) collective-permute-start(f32[2,64,128]{2,1,0:T(8,128)S(1)} %get-tuple-element.32), channel_id=1, source_target_pairs={{0,3},{1,2},{2,1},{3,0},{4,7},{5,6},{6,5},{7,4},{8,11},{9,10},{10,... | collective-permute-start | bytes 196616 | tf_op jit(solution)/shard_map/ppermute | solution.py:44
  39.0 6.4 %collective-permute-start.15 = (f32[2,128,128]{2,1,0:T(8,128)S(1)}, f32[2,128,128]{2,1,0:T(8,128)S(1)}, u32[]{:S(2)}, u32[]{:S(2)}) collective-permute-start(f32[2,128,128]{2,1,0:T(8,128)S(1)} %get-tuple-element.34), channel_id=1, source_target_pairs={{0,1},{1,0},{2,3},{3,2},{4,5},{5,4},{6,7},{7,6},{8,9},{9,8},{10,11... | collective-permute-start | bytes 393224 | tf_op jit(solution)/shard_map/ppermute | solution.py:44
  39.3 11.8 %collective-permute-start.16 = (f32[2,128,128]{2,1,0:T(8,128)S(1)}, f32[2,128,128]{2,1,0:T(8,128)S(1)}, u32[]{:S(2)}, u32[]{:S(2)}) collective-permute-start(f32[2,128,128]{2,1,0:T(8,128)S(1)} %get-tuple-element.35), channel_id=1, source_target_pairs={{0,2},{1,3},{2,0},{3,1},{4,6},{5,7},{6,4},{7,5},{8,10},{9,11},{10,... | collective-permute-start | bytes 393224 | tf_op jit(solution)/shard_map/ppermute | solution.py:44
  41.6 12.6 %collective-permute-start.17 = (f32[2,128,128]{2,1,0:T(8,128)S(1)}, f32[2,128,128]{2,1,0:T(8,128)S(1)}, u32[]{:S(2)}, u32[]{:S(2)}) collective-permute-start(f32[2,128,128]{2,1,0:T(8,128)S(1)} %get-tuple-element.36), channel_id=1, source_target_pairs={{0,3},{1,2},{2,1},{3,0},{4,7},{5,6},{6,5},{7,4},{8,11},{9,10},{10,... | collective-permute-start | bytes 393224 | tf_op jit(solution)/shard_map/ppermute | solution.py:44
